TPU v7x, 32 devices: a whole 2x2x4 slice. The times are simulated.
32 devices in a mesh: seq: 4 (over z), head: 4 (over y, x), batch: 2 (over core).
Axes of the slice: x: 2, y: 2, z: 4, core: 2. Of those that a mesh axis runs over, the one named last changes fastest.
Arguments:
- ssm_input: bfloat16 [16384, 5120], P(('batch', 'seq'), 'head'), parts along dimension 0, may hold values from -500 to 500
- gate_input: bfloat16 [16384, 5120], P(('batch', 'seq'), 'head'), parts along dimension 0, may hold values from -6 to 6
- b_proj: bfloat16 [16384, 1024], P(('batch', 'seq')), parts along dimension 0, may hold values from -2 to 2
- c_proj: bfloat16 [16384, 1024], P(('batch', 'seq')), parts along dimension 0, may hold values from -2 to 2
- step_size: float32 [80, 16384], P('head', ('batch', 'seq')), parts along dimension 1, may hold values from 0.02 to 0.2
- log_decay: float32 [80, 16384], P('head', ('batch', 'seq')), parts along dimension 1, may hold values from -1.5 to 0, as said below
- skip_gain: float32 [80], P('head'), may hold values from 0.5 to 1.5
- norm_gain: float32 [5120], replicated, may hold values from 0.1 to 1.9
- out_weight: bfloat16 [5120, 2560], P('head'), may hold values from -0.078125 to 0.078125
Outputs:
- layer_out: bfloat16 [16384, 2560], P(('batch', 'seq', 'head')), parts along dimension 0
There are 2 independent parts, one for each index of `batch`. A program takes and returns all parts, laid end to end along the dimension named above; an argument that names none is the same for every part. Nothing has to cross between parts.
Inputs may be any that keep to these rules, and one draw needn't show every extreme that they name: `log_decay`: negative.
All inputs are finite; a program needn't handle non-finite values.
Results may differ from a plain program's by a relative error of at most 0.018.
Values may be sent and summed in bfloat16 or wider, within the bound.
A program may use at most 192 MiB of HBM per device.

v0:
```python
import functools
import jax
import jax.numpy as jnp
from jax import lax
from jax.experimental import pallas as pl
from jax.experimental.pallas import tpu as pltpu
from jax.sharding import PartitionSpec as P

HEAD_COUNT = 80
HEAD_DIM = 64
STATE = 128
GROUPS = 8
BLOCK = 256
LANES = 128
epsilon = 1e-05
HIGHEST = lax.Precision.HIGHEST
F32 = jnp.float32
BF16 = jnp.bfloat16


def dot(a, b, ca, cb, precision=None):
    return lax.dot_general(
        a, b, (((ca,), (cb,)), ((), ())), precision=precision, preferred_element_type=F32
    )


def iotas(rows, columns):
    return (
        lax.broadcasted_iota(jnp.int32, (rows, columns), 0),
        lax.broadcasted_iota(jnp.int32, (rows, columns), 1),
    )


def lower_ones():
    t, s = iotas(BLOCK, BLOCK)
    return jnp.where(s <= t, 1.0, 0.0).astype(F32)


def identity():
    t, s = iotas(BLOCK, BLOCK)
    return jnp.where(s == t, 1.0, 0.0).astype(F32)


def pieces(channels, repeats):
    found = []
    for start in range(0, channels, LANES):
        width = min(LANES, channels - start)
        heads = [start // HEAD_DIM + i for i in range(width // HEAD_DIM)]
        found.append((start, width, heads, heads[0] // repeats))
    return found


def spread(columns, heads, width):
    first = jnp.broadcast_to(columns[:, heads[0] : heads[0] + 1], (BLOCK, width))
    if len(heads) == 1:
        return first
    second = jnp.broadcast_to(columns[:, heads[1] : heads[1] + 1], (BLOCK, width))
    lane = iotas(BLOCK, width)[1]
    return jnp.where(lane < HEAD_DIM, first, second)


def state_kernel(
    repeats, at_ref, x_ref, b_ref, step_ref, log_ref, prefix_ref, base_ref, total_ref, all_ref, s_ref, l_ref
):
    k = pl.program_id(0)
    channels = x_ref.shape[1]

    @pl.when(k == 0)
    def _():
        s_ref[...] = jnp.zeros_like(s_ref)
        l_ref[...] = jnp.zeros_like(l_ref)

    columns = dot(lower_ones(), log_ref[...], 1, 1, HIGHEST)
    steps = dot(identity(), step_ref[...], 1, 1, HIGHEST)
    base_ref[0] = l_ref[...]
    prefix_ref[0] = s_ref[...].astype(BF16)
    for start, width, heads, group in pieces(channels, repeats):
        lanes = pl.ds(start, width)
        cum = spread(columns, heads, width)
        last = cum[BLOCK - 1 : BLOCK, :]
        weighted = (
            x_ref[:, lanes].astype(F32) * (jnp.exp(last - cum) * spread(steps, heads, width))
        ).astype(BF16)
        new = dot(b_ref[:, group * STATE : (group + 1) * STATE], weighted, 0, 0)
        s_ref[:, lanes] = jnp.exp(last) * s_ref[:, lanes] + new
        l_ref[:, lanes] = l_ref[:, lanes] + last
    total_ref[...] = s_ref[...]
    all_ref[...] = jnp.exp(l_ref[...])


def within_kernel(
    repeats, at_ref, x_ref, b_ref, c_ref, step_ref, log_ref, skip_ref, prefix_ref, y_ref
):
    channels = x_ref.shape[1]
    half = BLOCK // 2
    lower = lower_ones()
    columns = dot(lower, log_ref[...], 1, 1, HIGHEST)
    rows = dot(log_ref[...], lower, 1, 1, HIGHEST) - jnp.log(step_ref[...])
    scores = {}
    for start, width, heads, group in pieces(channels, repeats):
        lanes = pl.ds(start, width)
        c_here = c_ref[:, group * STATE : (group + 1) * STATE]
        if group not in scores:
            full = dot(c_here, b_ref[:, group * STATE : (group + 1) * STATE], 1, 1)
            scores[group] = full * lower
        x_here = x_ref[:, lanes]
        lane = iotas(BLOCK, width)[1]
        top, bottom = 0.0, 0.0
        for i, head in enumerate(heads):
            kept = (lane >= i * HEAD_DIM) & (lane < (i + 1) * HEAD_DIM)
            x_head = x_here if len(heads) == 1 else jnp.where(kept, x_here, jnp.zeros_like(x_here))
            column, row = columns[:, head : head + 1], rows[head : head + 1, :]
            w_top = scores[group][:half, :half] * jnp.exp(
                jnp.minimum(column[:half] - row[:, :half], 0.0)
            )
            w_bottom = scores[group][half:] * jnp.exp(jnp.minimum(column[half:] - row, 0.0))
            top = top + dot(w_top.astype(BF16), x_head[:half], 1, 0)
            bottom = bottom + dot(w_bottom.astype(BF16), x_head, 1, 0)
        across = jnp.exp(spread(columns, heads, width)) * dot(c_here, prefix_ref[0, :, lanes], 1, 0)
        rest = across + skip_ref[:, lanes] * x_here.astype(F32)
        y_ref[:half, lanes] = (top + rest[:half]).astype(BF16)
        y_ref[half:, lanes] = (bottom + rest[half:]).astype(BF16)


def finish_kernel(
    repeats, at_ref, y_ref, gate_ref, c_ref, log_ref, base_ref, in_ref, gain_ref, w_ref, out_ref, sq_ref, g_ref
):
    channels = y_ref.shape[1]
    columns = dot(lower_ones(), log_ref[...], 1, 1, HIGHEST)
    squares = jnp.zeros((8, BLOCK), F32)
    for start, width, heads, group in pieces(channels, repeats):
        lanes = pl.ds(start, width)
        grow = jnp.exp(spread(columns, heads, width) + base_ref[0, 0:1, lanes])
        across = grow * dot(c_ref[:, group * STATE : (group + 1) * STATE], in_ref[:, lanes], 1, 0)
        gate = gate_ref[:, lanes].astype(F32)
        gated = (y_ref[:, lanes].astype(F32) + across) * (gate / (1.0 + jnp.exp(-gate)))
        squares = squares + dot(jnp.ones((8, width), BF16), (gated * gated).astype(BF16), 1, 1)
        g_ref[:, lanes] = (gated * gain_ref[:, lanes]).astype(BF16)
    sq_ref[...] = squares
    model = w_ref.shape[1]
    tile = 512 if model % 512 == 0 else model
    for start in range(0, model, tile):
        out_ref[:, start : start + tile] = dot(
            g_ref[...], w_ref[:, start : start + tile], 1, 0
        ).astype(BF16)


def shifted(value, axis, steps):
    count = lax.axis_size(axis)
    return lax.ppermute(value, axis, [(source, source + steps) for source in range(count - steps)])


def body(
    ssm_input, gate_input, b_proj, c_proj, step_size, log_decay, skip_gain, norm_gain, out_weight
):
    tokens, channels = ssm_input.shape
    heads = step_size.shape[0]
    blocks = tokens // BLOCK
    model = out_weight.shape[1]
    per_group = HEAD_COUNT // GROUPS
    groups = max(1, heads // per_group)
    repeats = min(heads, per_group)
    head_index = lax.axis_index("head")
    at = (head_index * heads // per_group // groups).astype(jnp.int32).reshape(1)
    skip = jnp.repeat(skip_gain, HEAD_DIM)[None, :]
    gain = lax.dynamic_slice_in_dim(norm_gain, head_index * channels, channels)[None, :]
    params = pltpu.CompilerParams(
        dimension_semantics=("arbitrary",), vmem_limit_bytes=56 * 1024 * 1024
    )

    def rows_of(width):
        return pl.BlockSpec((BLOCK, width), lambda k, at: (k, 0))

    grouped = pl.BlockSpec((BLOCK, groups * STATE), lambda k, at: (k, at[0]))
    head_rows = pl.BlockSpec((heads, BLOCK), lambda k, at: (0, k))
    fixed = lambda r, c: pl.BlockSpec((r, c), lambda k, at: (0, 0))
    state_block = pl.BlockSpec((1, STATE, channels), lambda k, at: (k, 0, 0))

    prefix, base, total, decay = pl.pallas_call(
        functools.partial(state_kernel, repeats),
        grid_spec=pltpu.PrefetchScalarGridSpec(
            num_scalar_prefetch=1,
            grid=(blocks,),
            in_specs=[rows_of(channels), grouped, head_rows, head_rows],
            out_specs=[
                state_block,
                pl.BlockSpec((1, 8, channels), lambda k, at: (k, 0, 0)),
                fixed(STATE, channels),
                fixed(8, channels),
            ],
            scratch_shapes=[pltpu.VMEM((STATE, channels), F32), pltpu.VMEM((8, channels), F32)],
        ),
        out_shape=[
            jax.ShapeDtypeStruct((blocks, STATE, channels), BF16),
            jax.ShapeDtypeStruct((blocks, 8, channels), F32),
            jax.ShapeDtypeStruct((STATE, channels), F32),
            jax.ShapeDtypeStruct((8, channels), F32),
        ],
        compiler_params=params,
        name="block_states",
        cost_estimate=pl.CostEstimate(
            flops=2 * tokens * channels * STATE, bytes_accessed=tokens * channels * 4, transcendentals=0
        ),
    )(at, ssm_input, b_proj, step_size, log_decay)

    incoming = shifted(total.astype(BF16), "seq", 1)
    for _ in range(lax.axis_size("seq") - 2):
        incoming = shifted((decay[0:1] * incoming.astype(F32) + total).astype(BF16), "seq", 1)

    shares = lax.axis_size("head")
    per_share = tokens // shares
    chunks = max(1, per_share // BLOCK)
    steps = blocks // chunks
    parts, squares = [], []
    for chunk in range(chunks):
        pick = lambda d, chunk=chunk: d * chunks + chunk
        picked = lambda width, pick=pick: pl.BlockSpec((BLOCK, width), lambda d, at: (pick(d), 0))
        y = pl.pallas_call(
            functools.partial(within_kernel, repeats),
            grid_spec=pltpu.PrefetchScalarGridSpec(
                num_scalar_prefetch=1,
                grid=(steps,),
                in_specs=[
                    picked(channels),
                    pl.BlockSpec((BLOCK, groups * STATE), lambda d, at: (pick(d), at[0])),
                    pl.BlockSpec((BLOCK, groups * STATE), lambda d, at: (pick(d), at[0])),
                    pl.BlockSpec((heads, BLOCK), lambda d, at: (0, pick(d))),
                    pl.BlockSpec((heads, BLOCK), lambda d, at: (0, pick(d))),
                    fixed(1, channels),
                    pl.BlockSpec((1, STATE, channels), lambda d, at: (pick(d), 0, 0)),
                ],
                out_specs=rows_of(channels),
            ),
            out_shape=jax.ShapeDtypeStruct((steps * BLOCK, channels), BF16),
            compiler_params=params,
            name="within",
            cost_estimate=pl.CostEstimate(
                flops=16 * steps * BLOCK * channels * BLOCK, bytes_accessed=steps * BLOCK * channels * 8, transcendentals=0
            ),
        )(at, ssm_input, b_proj, c_proj, step_size, log_decay, skip, prefix)
        partial, square = pl.pallas_call(
            functools.partial(finish_kernel, repeats),
            grid_spec=pltpu.PrefetchScalarGridSpec(
                num_scalar_prefetch=1,
                grid=(steps,),
                in_specs=[
                    rows_of(channels),
                    picked(channels),
                    pl.BlockSpec((BLOCK, groups * STATE), lambda d, at: (pick(d), at[0])),
                    pl.BlockSpec((heads, BLOCK), lambda d, at: (0, pick(d))),
                    pl.BlockSpec((1, 8, channels), lambda d, at: (pick(d), 0, 0)),
                    fixed(STATE, channels),
                    fixed(1, channels),
                    fixed(channels, model),
                ],
                out_specs=[
                    pl.BlockSpec((BLOCK, model), lambda d, at: (d, 0)),
                    pl.BlockSpec((8, BLOCK), lambda d, at: (0, d)),
                ],
                scratch_shapes=[pltpu.VMEM((BLOCK, channels), BF16)],
            ),
            out_shape=[
                jax.ShapeDtypeStruct((steps * BLOCK, model), BF16),
                jax.ShapeDtypeStruct((8, steps * BLOCK), F32),
            ],
            compiler_params=params,
            name="finish",
            cost_estimate=pl.CostEstimate(
                flops=2 * steps * BLOCK * channels * model,
                bytes_accessed=steps * BLOCK * (channels * 4 + model * 2) + channels * model * 2,
                transcendentals=0,
            ),
        )(at, y, gate_input, c_proj, log_decay, base, incoming, gain, out_weight)
        parts.append(lax.psum_scatter(partial, "head", scatter_dimension=0, tiled=True))
        squares.append(square[0].reshape(shares, per_share // chunks))
    squares = lax.psum_scatter(
        jnp.concatenate(squares, axis=1), "head", scatter_dimension=0, tiled=True
    ).reshape(per_share, 1)
    scale = lax.rsqrt(squares / (HEAD_COUNT * HEAD_DIM) + epsilon)
    return (jnp.concatenate(parts, axis=0).astype(F32) * scale).astype(BF16)


def solution(mesh):
    in_specs = (
        P(("batch", "seq"), "head"),
        P(("batch", "seq"), "head"),
        P(("batch", "seq"), None),
        P(("batch", "seq"), None),
        P("head", ("batch", "seq")),
        P("head", ("batch", "seq")),
        P("head"),
        P(),
        P("head", None),
    )
    out_specs = P(("batch", "seq", "head"), None)
    return jax.shard_map(body, mesh=mesh, in_specs=in_specs, out_specs=out_specs, check_vma=False)
```

profile of v0, /device:TPU:24, one launch (start us, length us, event | category | flops | bytes accessed | tf_op | source)
XLA Modules:
  0.0 224.8 jit_solution(18260190997612217312)
XLA Ops:
  6.5 0.0 reduce-scatter.3.cloned.1.call-start
  6.5 0.0 copy-start
  6.5 21.3 %block_states.1 = (bf16[8,128,1280]{2,1,0:T(8,128)(2,1)}, f32[8,8,1280]{2,1,0:T(8,128)}, f32[128,1280]{1,0:T(8,128)}, f32[8,1280]{1,0:T(8,128)}) custom-call(s32[1]{0:T(128)} %bitcast.at_ref, bf16[2048,1280]{1,0:T(8,128)(2,1)} %x_ref.5, bf16[2048,1024]{1,0:T(8,128)(2,1)} %b_ref.5, f32[20,2048]{1,0:T(8,128)} %step_ref.5, f32[20,2048]{1,0:T(8,128)} %log_ref.9), custom_call_target="tpu_custom_call" | custom-call | flops 671088640 | bytes 10485760 | tf_op jit(solution)/shard_map/block_states/pallas_call | solution.py:179
  27.8 1.1 convert_element_type.21
  29.0 1.3 collective-permute-start
  30.3 0.8 slice_reduce_fusion
  31.1 9.2 %collective-permute-done = bf16[128,1280]{1,0:T(8,128)(2,1)S(1)} collective-permute-done((bf16[128,1280]{1,0:T(8,128)(2,1)S(1)}, bf16[128,1280]{1,0:T(8,128)(2,1)S(1)}, u32[]{:S(2)}, u32[]{:S(2)}) %collective-permute-start) | collective-permute-done | bytes 327712 | tf_op jit(solution)/shard_map/ppermute | solution.py:150
  40.3 1.2 add_convert_fusion.1
  41.5 1.3 collective-permute-start.1
  42.8 0.8 dynamic_slice.3
  43.6 0.6 broadcast_in_dim.7.gain_ref
  44.2 0.0 copy-done
  44.2 0.1 broadcast_in_dim.6
  44.2 0.7 broadcast_in_dim_reshape.3.skip_ref
  44.9 7.1 %collective-permute-done.1 = bf16[128,1280]{1,0:T(8,128)(2,1)S(1)} collective-permute-done((bf16[128,1280]{1,0:T(8,128)(2,1)S(1)}, bf16[128,1280]{1,0:T(8,128)(2,1)S(1)}, u32[]{:S(2)}, u32[]{:S(2)}) %collective-permute-start.1) | collective-permute-done | bytes 327712 | tf_op jit(solution)/shard_map/ppermute | solution.py:150
  52.0 1.2 add_convert_fusion
  53.1 1.3 collective-permute-start.2
  54.4 10.7 %within.2.y_ref = bf16[1024,1280]{1,0:T(8,128)(2,1)} custom-call(s32[1]{0:T(128)} %bitcast.at_ref, bf16[2048,1280]{1,0:T(8,128)(2,1)} %x_ref.5, bf16[2048,1024]{1,0:T(8,128)(2,1)} %b_ref.5, bf16[2048,1024]{1,0:T(8,128)(2,1)} %c_ref.7, f32[20,2048]{1,0:T(8,128)} %step_ref.5, f32[20,2048]{1,0:T(8,128)} %log_ref.9, f32[1,1280]{1,0:T(1,128)} %broadcast_in_dim_reshape.3.skip_ref, ...), custom_call_target="tpu_custom_call" | custom-call | flops 5368709120 | bytes 10485760 | tf_op jit(solution)/shard_map/within/pallas_call | solution.py:218
  65.2 0.0 collective-permute-done.2.in_ref
  65.2 0.0 copy-start.1
  65.2 0.7 copy-done.1
  66.0 19.9 %finish.2 = (bf16[1024,2560]{1,0:T(8,128)(2,1)}, f32[8,1024]{1,0:T(8,128)}) custom-call(s32[1]{0:T(128)} %bitcast.at_ref, bf16[1024,1280]{1,0:T(8,128)(2,1)} %within.2.y_ref, bf16[2048,1280]{1,0:T(8,128)(2,1)} %gate_ref.3, bf16[2048,1024]{1,0:T(8,128)(2,1)} %c_ref.7, f32[20,2048]{1,0:T(8,128)} %log_ref.9, f32[8,8,1280]{2,1,0:T(8,128)} %get-tuple-element.14.base_ref, ...), custom_call_target="tpu_custom_call" | custom-call | flops 6710886400 | bytes 17039360 | tf_op jit(solution)/shard_map/finish/pallas_call | solution.py:241
  85.9 0.0 reduce-scatter.3.cloned.1.call-update
  85.9 0.2 reduce-scatter.5.cloned.1.call-start
  86.1 10.7 %within.3.y_ref = bf16[1024,1280]{1,0:T(8,128)(2,1)} custom-call(s32[1]{0:T(128)} %bitcast.at_ref, bf16[2048,1280]{1,0:T(8,128)(2,1)} %x_ref.5, bf16[2048,1024]{1,0:T(8,128)(2,1)} %b_ref.5, bf16[2048,1024]{1,0:T(8,128)(2,1)} %c_ref.7, f32[20,2048]{1,0:T(8,128)} %step_ref.5, f32[20,2048]{1,0:T(8,128)} %log_ref.9, f32[1,1280]{1,0:T(1,128)} %broadcast_in_dim_reshape.3.skip_ref, ...), custom_call_target="tpu_custom_call" | custom-call | flops 5368709120 | bytes 10485760 | tf_op jit(solution)/shard_map/within/pallas_call | solution.py:218
  96.9 19.9 %finish.3 = (bf16[1024,2560]{1,0:T(8,128)(2,1)}, f32[8,1024]{1,0:T(8,128)}) custom-call(s32[1]{0:T(128)} %bitcast.at_ref, bf16[1024,1280]{1,0:T(8,128)(2,1)} %within.3.y_ref, bf16[2048,1280]{1,0:T(8,128)(2,1)} %gate_ref.3, bf16[2048,1024]{1,0:T(8,128)(2,1)} %c_ref.7, f32[20,2048]{1,0:T(8,128)} %log_ref.9, f32[8,8,1280]{2,1,0:T(8,128)} %get-tuple-element.14.base_ref, ...), custom_call_target="tpu_custom_call" | custom-call | flops 6710886400 | bytes 17039360 | tf_op jit(solution)/shard_map/finish/pallas_call | solution.py:241
  116.8 0.0 copy-start.2
  116.8 0.0 reduce-scatter.5.cloned.1.call-update
  116.8 0.6 copy-done.2
  117.5 0.6 dynamic-slice
  118.1 0.8 slice_reduce_fusion.2
  118.9 0.8 slice_reduce_fusion.1
  119.7 10.1 %all-reduce = f32[4,512]{1,0:T(4,128)S(1)} all-reduce(f32[4,512]{1,0:T(4,128)S(1)} %pad_maximum_fusion), channel_id=4, replica_groups=mesh['seq'=4,'head'=4,'batch'=2] {'head'}, use_global_device_ids=true, to_apply=%region_2.3.clone | all-reduce | flops 2048 | bytes 16384
  129.8 0.7 fusion.1
  130.5 19.5 %reduce-scatter.3.cloned.1.call-done = bf16[256,2560]{1,0:T(8,128)(2,1)} async-done(((bf16[1024,2560]{1,0:T(8,128)(2,1)}), bf16[256,2560]{1,0:T(8,128)(2,1)}) %reduce-scatter.3.cloned.1.call-update) | async-done | bytes 1310736 | tf_op jit(solution)/shard_map/reduce_scatter | solution.py:274
  149.9 64.3 %reduce-scatter.5.cloned.1.call-done = bf16[256,2560]{1,0:T(8,128)(2,1)} async-done(((bf16[1024,2560]{1,0:T(8,128)(2,1)}), bf16[256,2560]{1,0:T(8,128)(2,1)}) %reduce-scatter.5.cloned.1.call-update) | async-done | bytes 1310736 | tf_op jit(solution)/shard_map/reduce_scatter | solution.py:274
  214.2 3.7 %multiply_convert_fusion = bf16[512,2560]{1,0:T(8,128)(2,1)} fusion(bf16[256,2560]{1,0:T(8,128)(2,1)} %reduce-scatter.5.cloned.1.call-done, bf16[256,2560]{1,0:T(8,128)(2,1)} %reduce-scatter.3.cloned.1.call-done, f32[512]{0:T(512)S(1)} %bitcast.3), kind=kLoop, calls=%fused_computation | loop fusion | flops 7864320 | bytes 5244928 | tf_op jit(solution)/shard_map/convert_element_type | solution.py:280
  (3 shorter events, 0.0 us)
Async XLA Ops:
  6.5 143.4 %reduce-scatter.3.cloned.1.call-start = ((), (), s32[]{:S(2)}) async-start(), calls=%async_computation.2 | async-start | bytes 6553600 | tf_op jit(solution)/shard_map/reduce_scatter | solution.py:274
  6.5 37.6 %copy-start = (f32[20]{0:T(128)S(1)}, f32[20]{0:T(128)}, u32[]{:S(2)}) copy-start(f32[20]{0:T(128)} %param.15) | copy-start | bytes 244
  29.0 11.3 %collective-permute-start = (bf16[128,1280]{1,0:T(8,128)(2,1)S(1)}, bf16[128,1280]{1,0:T(8,128)(2,1)S(1)}, u32[]{:S(2)}, u32[]{:S(2)}) collective-permute-start(bf16[128,1280]{1,0:T(8,128)(2,1)S(1)} %convert_element_type.21), channel_id=1, source_target_pairs={{0,8},{8,16},{16,24},{1,9},{9,17},{17,25},{2,10},{10,18},{18,26},{... | collective-permute-start | bytes 983048 | tf_op jit(solution)/shard_map/ppermute | solution.py:150
  41.5 10.5 %collective-permute-start.1 = (bf16[128,1280]{1,0:T(8,128)(2,1)S(1)}, bf16[128,1280]{1,0:T(8,128)(2,1)S(1)}, u32[]{:S(2)}, u32[]{:S(2)}) collective-permute-start(bf16[128,1280]{1,0:T(8,128)(2,1)S(1)} %add_convert_fusion.1), channel_id=1, source_target_pairs={{0,8},{8,16},{16,24},{1,9},{9,17},{17,25},{2,10},{10,18},{18,26},{... | collective-permute-start | bytes 983048 | tf_op jit(solution)/shard_map/ppermute | solution.py:150
  53.1 12.1 %collective-permute-start.2 = (bf16[128,1280]{1,0:T(8,128)(2,1)S(1)}, bf16[128,1280]{1,0:T(8,128)(2,1)S(1)}, u32[]{:S(2)}, u32[]{:S(2)}) collective-permute-start(bf16[128,1280]{1,0:T(8,128)(2,1)S(1)} %add_convert_fusion), channel_id=1, source_target_pairs={{0,8},{8,16},{16,24},{1,9},{9,17},{17,25},{2,10},{10,18},{18,26},{... | collective-permute-start | bytes 983048 | tf_op jit(solution)/shard_map/ppermute | solution.py:150
  65.2 0.8 copy-start.1
  85.9 128.3 %reduce-scatter.5.cloned.1.call-start = ((), (), s32[]{:S(2)}) async-start(), calls=%async_computation.3 | async-start | bytes 6553600 | tf_op jit(solution)/shard_map/reduce_scatter | solution.py:274
  116.8 0.7 copy-start.2
Sparse Core Ops, SparseCore 0:
  86.0 63.8 reduce-scatter.2
  152.9 61.2 reduce-scatter.4
where the time goes:
time: 227 us; the launch traced here: 225 us
  waiting for transfers between devices  100 us (44%)
  Pallas kernels  82.6 us (36%)
  between operations  13.5 us (6%)
  blocking collectives  10.1 us (4%)
  other arithmetic  7.83 us (3%)
  local copies, waits for them, and re-layouts  6.51 us (3%)
  starting transfers between devices  4.1 us (2%)
    reduce_scatter x2, waiting for transfers between devices, body(): lax.psum_scatter(partial, 'head', scatter_dimension=0, tiled=True)  83.8 us
    pallas_call x2, Pallas kernels, body(): pl.pallas_call(functools.partial(finish_kernel, repeats), grid_spec=pltpu...  39.9 us
    pallas_call x2, Pallas kernels, body(): pl.pallas_call(functools.partial(within_kernel, repeats), grid_spec=pltpu...  21.5 us
    pallas_call x1, Pallas kernels, body(): pl.pallas_call(functools.partial(state_kernel, repeats), grid_spec=pltpu....  21.3 us
    ppermute x3, waiting for transfers between devices, shifted(): lax.ppermute(value, axis, [(source, source + steps) for source in range(c...  16.3 us
    unnamed x1, blocking collectives  10.1 us
  transfers between devices with their start and end apart: 5, of which 4 were waited for; matrix products, arithmetic and copies ran while one was open for 3% of the time, Pallas kernels for 18%

commit v1 on v0

v1 whole, which is shorter than its diff:
```python
import functools
import jax
import jax.numpy as jnp
from jax import lax
from jax.experimental import pallas as pl
from jax.experimental.pallas import tpu as pltpu
from jax.sharding import PartitionSpec as P

HEAD_COUNT = 80
HEAD_DIM = 64
STATE = 128
GROUPS = 8
BLOCK = 256
LANES = 128
UNIT = 128
epsilon = 1e-05
HIGHEST = lax.Precision.HIGHEST
F32 = jnp.float32
BF16 = jnp.bfloat16
MESH = pl.DeviceIdType.MESH


def dot(a, b, ca, cb, precision=None):
    return lax.dot_general(
        a, b, (((ca,), (cb,)), ((), ())), precision=precision, preferred_element_type=F32
    )


def iotas(rows, columns):
    return (
        lax.broadcasted_iota(jnp.int32, (rows, columns), 0),
        lax.broadcasted_iota(jnp.int32, (rows, columns), 1),
    )


def pieces(channels, repeats):
    found = []
    for start in range(0, channels, LANES):
        width = min(LANES, channels - start)
        heads = [start // HEAD_DIM + i for i in range(width // HEAD_DIM)]
        found.append((len(found), start, width, heads, heads[0] // repeats))
    return found


def spread(columns, heads, width):
    rows = columns.shape[0]
    first = jnp.broadcast_to(columns[:, heads[0] : heads[0] + 1], (rows, width))
    if len(heads) == 1:
        return first
    second = jnp.broadcast_to(columns[:, heads[1] : heads[1] + 1], (rows, width))
    lane = iotas(rows, width)[1]
    return jnp.where(lane < HEAD_DIM, first, second)


def split(value, count):
    parts = []
    for _ in range(count):
        part = value.astype(BF16)
        parts.append(part)
        value = value - part.astype(F32)
    return parts


def column_tiles(start, stop, size):
    return [(at, min(size, stop - at)) for at in range(start, stop, size)]


def mixer_kernel(
    plan, x_hbm, gate_hbm, b_hbm, c_hbm, step_hbm, log_hbm, skip_ref, gain_ref, w_hbm, out_hbm,
    x, gate, b, c, step, log, w, stack, stack2, rows_ref, cols_ref, wcols_ref, prefix, base,
    state_out, state_in, g_ref, part, squares, squares_in, first_a, first_b, second_a, second_b, stage,
    load_sem, out_sem, state_send, state_recv, square_send, square_recv,
    first_a_send, first_a_recv, first_b_send, first_b_recv,
    second_a_send, second_a_recv, second_b_send, second_b_recv,
):
    X, Y, S, groups, repeats = plan
    H = X * Y
    tokens, channels = x.shape
    model = w.shape[1]
    half = model // 2
    heads = step.shape[0]
    padded = stack.shape[0] // (tokens // BLOCK)
    blocks = tokens // BLOCK
    per_share = tokens // H
    unit = min(UNIT, per_share)
    subs = per_share // unit
    units = BLOCK // unit
    per_group = HEAD_COUNT // GROUPS
    every = pieces(channels, repeats)

    me = lax.axis_index("head")
    z = lax.axis_index("seq")
    gx = me % X
    gy = me // X
    to = lambda dx, dy: {"head": ((gy + dy) % Y) * X + (gx + dx) % X}
    after = {"seq": lax.rem(z + 1, S)}

    offset = pl.multiple_of((me * heads // per_group) // groups * (groups * STATE), STATE)
    loads = [
        pltpu.make_async_copy(log_hbm, log, load_sem.at[0]),
        pltpu.make_async_copy(step_hbm, step, load_sem.at[1]),
        pltpu.make_async_copy(b_hbm.at[:, pl.ds(offset, groups * STATE)], b, load_sem.at[2]),
        pltpu.make_async_copy(x_hbm, x, load_sem.at[3]),
        pltpu.make_async_copy(c_hbm.at[:, pl.ds(offset, groups * STATE)], c, load_sem.at[4]),
        pltpu.make_async_copy(gate_hbm, gate, load_sem.at[5]),
        pltpu.make_async_copy(w_hbm, w, load_sem.at[6]),
    ]
    for load in loads:
        load.start()

    barrier = pltpu.get_barrier_semaphore()
    for d in range(1, H):
        pl.semaphore_signal(barrier, inc=1, device_id={"head": lax.rem(me + d, H)}, device_id_type=MESH)
    if S > 1:
        @pl.when(z > 0)
        def _():
            pl.semaphore_signal(barrier, inc=1, device_id={"seq": lax.max(z - 1, 0)}, device_id_type=MESH)

        @pl.when(z < S - 1)
        def _():
            pl.semaphore_signal(barrier, inc=1, device_id=after, device_id_type=MESH)

    near = 0
    if S > 1:
        near = jnp.where(z > 0, 1, 0) + jnp.where(z < S - 1, 1, 0)
    pl.semaphore_wait(barrier, near + (H - 1))

    def state_copy(p):
        return pltpu.make_async_remote_copy(
            src_ref=state_out.at[p], dst_ref=state_in.at[p], send_sem=state_send.at[p],
            recv_sem=state_recv.at[p], device_id=after, device_id_type=MESH,
        )

    t_iota, s_iota = iotas(BLOCK, BLOCK)
    lower = jnp.where(s_iota <= t_iota, 1.0, 0.0)
    lower_b = lower.astype(BF16)
    same_b = jnp.where(s_iota == t_iota, 1.0, 0.0).astype(BF16)
    stack[...] = jnp.zeros_like(stack)
    stack2[...] = jnp.ones_like(stack2)
    prefix[0] = jnp.zeros(prefix.shape[1:], F32)
    base[0:8] = jnp.zeros((8, channels), F32)
    state_out[...] = jnp.zeros_like(state_out)

    @pl.when(z == 0)
    def _():
        state_in[...] = jnp.zeros_like(state_in)

    loads[0].wait()
    loads[1].wait()
    for k in range(blocks):
        stack[k * padded : k * padded + heads, :] = log[:, k * BLOCK : (k + 1) * BLOCK]
        stack2[k * padded : k * padded + heads, :] = step[:, k * BLOCK : (k + 1) * BLOCK]
    rows_all, cols_all = 0.0, 0.0
    for part_of in split(stack[...], 3):
        rows_all = rows_all + dot(part_of, lower_b, 1, 1)
        cols_all = cols_all + dot(lower_b, part_of, 1, 1)
    steps = stack2[...]
    rows_ref[...] = rows_all - jnp.log(steps)
    to_end = jnp.exp(rows_all[:, BLOCK - 1 : BLOCK] - rows_all) * steps
    to_end_cols = 0.0
    for part_of in split(to_end, 2):
        to_end_cols = to_end_cols + dot(same_b, part_of, 1, 1)
    for k in range(blocks):
        cols_ref[k] = cols_all[:, k * padded : (k + 1) * padded]
        wcols_ref[k] = to_end_cols[:, k * padded : (k + 1) * padded]

    loads[2].wait()
    loads[3].wait()
    middle = (len(every) + 1) // 2
    for some in (every[:middle], every[middle:]):
        if not some:
            continue

        def state_step(k, carry, some=some):
            row = pl.ds(pl.multiple_of(k * BLOCK, BLOCK), BLOCK)
            spot = pl.ds(pl.multiple_of(k * 8, 8), 8)
            following = pl.ds(pl.multiple_of(k * 8 + 8, 8), 8)
            end = cols_ref[k, BLOCK - 8 : BLOCK, :][7:8, :]
            wide = wcols_ref[k]
            for p, start, width, of, group in some:
                lanes = slice(start, start + width)
                last = spread(end, of, width)
                weighted = (x[row, lanes].astype(F32) * spread(wide, of, width)).astype(BF16)
                new = dot(b[row, group * STATE : (group + 1) * STATE], weighted, 0, 0)
                prefix[k + 1, :, lanes] = jnp.exp(last) * prefix[k, :, lanes] + new
                base[following, lanes] = base[spot, lanes] + last
            return carry

        lax.fori_loop(0, blocks, state_step, 0)
        if S > 1:
            @pl.when(z == 0)
            def _(some=some):
                for p, start, width, of, group in some:
                    state_out[p, :, :width] = prefix[blocks, :, start : start + width].astype(BF16)
                    state_copy(p).start()

    def pass_state():
        for p, start, width, of, group in every:
            lanes = slice(start, start + width)
            state_copy(p).wait_recv()

            @pl.when(z < S - 1)
            def _():
                grown = jnp.exp(base[blocks * 8 : blocks * 8 + 1, lanes]) * state_in[p, :, :width].astype(F32)
                state_out[p, :, :width] = (grown + prefix[blocks, :, lanes]).astype(BF16)
                state_copy(p).start()

    def block_of(j):
        if per_share < BLOCK:
            return j
        chunks = per_share // BLOCK
        o = j // chunks
        dx = X - 1 - o // Y
        dy = Y - 1 - o % Y
        return (((gy + dy) % Y) * X + (gx + dx) % X) * chunks + j % chunks

    def within(j):
        k = block_of(j)
        row = pl.ds(pl.multiple_of(k * BLOCK, BLOCK), BLOCK)
        mid = BLOCK // 2
        columns = cols_ref[k]
        rows = rows_ref[pl.ds(pl.multiple_of(k * padded, padded), padded), :]
        scores = {}
        for p, start, width, of, group in every:
            lanes = slice(start, start + width)
            if group not in scores:
                which = slice(group * STATE, (group + 1) * STATE)
                scores[group] = dot(c[row, which], b[row, which], 1, 1) * lower
            x_here = x[row, lanes]
            lane = iotas(BLOCK, width)[1]
            top, bottom = 0.0, 0.0
            for i, head in enumerate(of):
                kept = (lane >= i * HEAD_DIM) & (lane < (i + 1) * HEAD_DIM)
                x_head = x_here if len(of) == 1 else jnp.where(kept, x_here, jnp.zeros_like(x_here))
                column, across = columns[:, head : head + 1], rows[head : head + 1, :]
                w_top = scores[group][:mid, :mid] * jnp.exp(
                    jnp.minimum(column[:mid] - across[:, :mid], 0.0)
                )
                w_bottom = scores[group][mid:] * jnp.exp(jnp.minimum(column[mid:] - across, 0.0))
                top = top + dot(w_top.astype(BF16), x_head[:mid], 1, 0)
                bottom = bottom + dot(w_bottom.astype(BF16), x_head, 1, 0)
            direct = skip_ref[:, lanes] * x_here.astype(F32)
            x[row, lanes] = jnp.concatenate([top + direct[:mid], bottom + direct[mid:]], axis=0).astype(BF16)

    def first_copy(buffer, send, recv, dx, dy, sub, row, columns, slot):
        return pltpu.make_async_remote_copy(
            src_ref=part.at[pl.ds(row, unit), columns],
            dst_ref=buffer.at[slot[0], slot[1], sub],
            send_sem=send.at[slot[0], slot[1], sub],
            recv_sem=recv.at[slot[0], slot[1], sub],
            device_id=to(dx, dy), device_id_type=MESH,
        )

    def copy_a(dx, dy, sub, row):
        return first_copy(
            first_a, first_a_send, first_a_recv, dx, 0, sub, row, pl.ds(0, half), (dx - 1, dy)
        )

    def copy_b(dx, dy, sub, row):
        return first_copy(
            first_b, first_b_send, first_b_recv, 0, dy, sub, row, pl.ds(half, model - half), (dy - 1, dx)
        )

    def copy_squares(dx, dy, sub, index):
        slot = dx * Y + dy
        return pltpu.make_async_remote_copy(
            src_ref=squares.at[index], dst_ref=squares_in.at[slot, sub],
            send_sem=square_send.at[slot, sub], recv_sem=square_recv.at[slot, sub],
            device_id=to(dx, dy), device_id_type=MESH,
        )

    def finish(j):
        k = block_of(j)
        row = pl.ds(pl.multiple_of(k * BLOCK, BLOCK), BLOCK)
        grow_all = jnp.exp(cols_ref[k])
        before = jnp.exp(base[pl.ds(pl.multiple_of(k * 8, 8), 8), :])
        total = {}
        for p, start, width, of, group in every:
            lanes = slice(start, start + width)
            entering = prefix[k, :, lanes] + before[0:1, lanes] * state_in[p, :, :width].astype(F32)
            moved = dot(c[row, group * STATE : (group + 1) * STATE], entering.astype(BF16), 1, 0)
            across = spread(grow_all, of, width) * moved
            v = gate[row, lanes].astype(F32)
            gated = (x[row, lanes].astype(F32) + across) * (v * (0.5 + 0.5 * jnp.tanh(0.5 * v)))
            total[width] = total.get(width, 0.0) + gated * gated
            g_ref[:, lanes] = (gated * gain_ref[:, lanes]).astype(BF16)
        summed = jnp.zeros((8, BLOCK), F32)
        for width, value in total.items():
            for part_of in split(value, 2):
                summed = summed + dot(jnp.ones((8, width), BF16), part_of, 1, 1)
        for u in range(units):
            squares[k * units + u] = summed[:, u * unit : (u + 1) * unit]
        where = []
        for u in range(units):
            begin = pl.multiple_of(k * BLOCK + u * unit, unit)
            owner = begin // per_share
            sub = (begin % per_share) // unit
            where.append(((owner % X - gx + X) % X, (owner // X - gy + Y) % Y, sub, begin, k * units + u))
        for start, width in column_tiles(0, half, 512):
            part[row, start : start + width] = dot(g_ref[...], w[:, start : start + width], 1, 0).astype(BF16)
        for dx, dy, sub, begin, index in where:
            @pl.when(dx > 0)
            def _():
                copy_a(dx, dy, sub, begin).start()
        for start, width in column_tiles(half, model, 512):
            part[row, start : start + width] = dot(g_ref[...], w[:, start : start + width], 1, 0).astype(BF16)
        for dx, dy, sub, begin, index in where:
            @pl.when(dy > 0)
            def _():
                copy_b(dx, dy, sub, begin).start()

            @pl.when(dx + dy > 0)
            def _():
                copy_squares(dx, dy, sub, index).start()

    loads[4].wait()
    lag = max(1, (S - 1) * blocks // S) if S > 1 else 1
    waits = jnp.where(z > 0, lax.max(z * blocks // S, 1) - 1, -1) if S > 1 else None

    def main_step(i, carry):
        @pl.when(i < blocks)
        def _():
            within(i)

        if S > 1:
            @pl.when(i == waits)
            def _():
                pass_state()

        @pl.when(i == lag)
        def _():
            loads[5].wait()
            loads[6].wait()

        @pl.when(i >= lag)
        def _():
            finish(i - lag)

        return carry

    lax.fori_loop(0, blocks + lag, main_step, 0)

    def second_copy(buffer, send, recv, dx, dy, slot, sub, row, columns):
        return pltpu.make_async_remote_copy(
            src_ref=part.at[pl.ds(row, unit), columns], dst_ref=buffer.at[slot, sub],
            send_sem=send.at[slot, sub], recv_sem=recv.at[slot, sub],
            device_id=to(dx, dy), device_id_type=MESH,
        )

    left, right = pl.ds(0, half), pl.ds(half, model - half)

    def row_of(dx, dy, sub):
        owner = ((gy + dy) % Y) * X + (gx + dx) % X
        return pl.multiple_of(owner * per_share + sub * unit, unit)

    second_a_copy = lambda dy, sub: second_copy(
        second_a, second_a_send, second_a_recv, 0, dy, dy - 1, sub, row_of(0, dy, sub), left
    )
    second_b_copy = lambda dx, sub: second_copy(
        second_b, second_b_send, second_b_recv, dx, 0, dx - 1, sub, row_of(dx, 0, sub), right
    )

    def partial_sum(row, columns, buffer, copy, count, other, sub):
        value = part[pl.ds(row, unit), columns].astype(F32)
        for d in range(1, count):
            copy(d, other, sub, row).wait_recv()
            value = value + buffer[d - 1, other, sub].astype(F32)
        return value

    swapped_b = lambda dy, dx, sub, row: copy_b(dx, dy, sub, row)

    def relay(sub, carry):
        for dy in range(1, Y):
            row = row_of(0, dy, sub)
            part[pl.ds(row, unit), left] = partial_sum(row, left, first_a, copy_a, X, dy, sub).astype(BF16)
            second_a_copy(dy, sub).start()
        for dx in range(1, X):
            row = row_of(dx, 0, sub)
            part[pl.ds(row, unit), right] = partial_sum(row, right, first_b, swapped_b, Y, dx, sub).astype(BF16)
            second_b_copy(dx, sub).start()
        return carry

    lax.fori_loop(0, subs, relay, 0)

    def out_copy(sub):
        there = pl.ds(pl.multiple_of(sub * unit, unit), unit)
        return pltpu.make_async_copy(stage.at[there, :], out_hbm.at[there, :], out_sem.at[sub])

    same_u = jnp.where(iotas(unit, unit)[0] == iotas(unit, unit)[1], 1.0, 0.0)

    def settle(sub, carry):
        row = row_of(0, 0, sub)
        there = pl.ds(pl.multiple_of(sub * unit, unit), unit)
        summed = squares[me * subs + sub]
        for dx in range(X):
            for dy in range(Y):
                if dx + dy > 0:
                    copy_squares(dx, dy, sub, 0).wait_recv()
                    summed = summed + squares_in[dx * Y + dy, sub]
        column = dot(same_u, summed, 1, 1, HIGHEST)[:, 0:1]
        scale = lax.rsqrt(column / (HEAD_COUNT * HEAD_DIM) + epsilon)
        value = partial_sum(row, left, first_a, copy_a, X, 0, sub)
        for dy in range(1, Y):
            second_a_copy(dy, sub).wait_recv()
            value = value + second_a[dy - 1, sub].astype(F32)
        stage[there, left] = (value * scale).astype(BF16)
        value = partial_sum(row, right, first_b, swapped_b, Y, 0, sub)
        for dx in range(1, X):
            second_b_copy(dx, sub).wait_recv()
            value = value + second_b[dx - 1, sub].astype(F32)
        stage[there, right] = (value * scale).astype(BF16)
        out_copy(sub).start()
        return carry

    lax.fori_loop(0, subs, settle, 0)

    def drain(sub, carry):
        for dx in range(X):
            for dy in range(Y):
                if dx > 0:
                    copy_a(dx, dy, sub, 0).wait_send()
                if dy > 0:
                    copy_b(dx, dy, sub, 0).wait_send()
                if dx + dy > 0:
                    copy_squares(dx, dy, sub, 0).wait_send()
        for dy in range(1, Y):
            second_a_copy(dy, sub).wait_send()
        for dx in range(1, X):
            second_b_copy(dx, sub).wait_send()
        out_copy(sub).wait()
        return carry

    lax.fori_loop(0, subs, drain, 0)
    if S > 1:
        @pl.when(z < S - 1)
        def _():
            for p, start, width, of, group in every:
                state_copy(p).wait_send()


def body(
    ssm_input, gate_input, b_proj, c_proj, step_size, log_decay, skip_gain, norm_gain, out_weight
):
    tokens, channels = ssm_input.shape
    heads = step_size.shape[0]
    blocks = tokens // BLOCK
    model = out_weight.shape[1]
    half = model // 2
    per_group = HEAD_COUNT // GROUPS
    groups = max(1, heads // per_group)
    repeats = min(heads, per_group)
    H = lax.axis_size("head")
    S = lax.axis_size("seq")
    X = max(d for d in range(1, H + 1) if H % d == 0 and d * d <= H)
    Y = H // X
    per_share = tokens // H
    unit = min(UNIT, per_share)
    subs = per_share // unit
    count = len(pieces(channels, repeats))
    padded = -(-heads // 8) * 8
    head_index = lax.axis_index("head")
    skip = jnp.repeat(skip_gain, HEAD_DIM)[None, :]
    gain = lax.dynamic_slice_in_dim(norm_gain, head_index * channels, channels)[None, :]
    anywhere = pl.BlockSpec(memory_space=pl.ANY)
    vmem = pl.BlockSpec(memory_space=pltpu.VMEM)
    dma = pltpu.SemaphoreType.DMA
    x1, y1 = max(X - 1, 1), max(Y - 1, 1)
    return pl.pallas_call(
        functools.partial(mixer_kernel, (X, Y, S, groups, repeats)),
        in_specs=[anywhere] * 6 + [vmem, vmem, anywhere],
        out_specs=anywhere,
        out_shape=jax.ShapeDtypeStruct((per_share, model), BF16),
        scratch_shapes=[
            pltpu.VMEM((tokens, channels), BF16),
            pltpu.VMEM((tokens, channels), BF16),
            pltpu.VMEM((tokens, groups * STATE), BF16),
            pltpu.VMEM((tokens, groups * STATE), BF16),
            pltpu.VMEM((heads, tokens), F32),
            pltpu.VMEM((heads, tokens), F32),
            pltpu.VMEM((channels, model), BF16),
            pltpu.VMEM((blocks * padded, BLOCK), F32),
            pltpu.VMEM((blocks * padded, BLOCK), F32),
            pltpu.VMEM((blocks * padded, BLOCK), F32),
            pltpu.VMEM((blocks, BLOCK, padded), F32),
            pltpu.VMEM((blocks, BLOCK, padded), F32),
            pltpu.VMEM((blocks + 1, STATE, channels), F32),
            pltpu.VMEM(((blocks + 1) * 8, channels), F32),
            pltpu.VMEM((count, STATE, LANES), BF16),
            pltpu.VMEM((count, STATE, LANES), BF16),
            pltpu.VMEM((BLOCK, channels), BF16),
            pltpu.VMEM((tokens, model), BF16),
            pltpu.VMEM((tokens // unit, 8, unit), F32),
            pltpu.VMEM((H, subs, 8, unit), F32),
            pltpu.VMEM((x1, Y, subs, unit, half), BF16),
            pltpu.VMEM((y1, X, subs, unit, model - half), BF16),
            pltpu.VMEM((y1, subs, unit, half), BF16),
            pltpu.VMEM((x1, subs, unit, model - half), BF16),
            pltpu.VMEM((per_share, model), BF16),
            dma((7,)),
            dma((subs,)),
            dma((count,)),
            dma((count,)),
            dma((H, subs)),
            dma((H, subs)),
            dma((x1, Y, subs)),
            dma((x1, Y, subs)),
            dma((y1, X, subs)),
            dma((y1, X, subs)),
            dma((y1, subs)),
            dma((y1, subs)),
            dma((x1, subs)),
            dma((x1, subs)),
        ],
        compiler_params=pltpu.CompilerParams(
            collective_id=0, has_side_effects=True, vmem_limit_bytes=62 * 1024 * 1024
        ),
        name="mixer",
        cost_estimate=pl.CostEstimate(
            flops=2 * tokens * channels * (model + 4 * BLOCK), bytes_accessed=tokens * channels * 8, transcendentals=0
        ),
    )(ssm_input, gate_input, b_proj, c_proj, step_size, log_decay, skip, gain, out_weight)


def solution(mesh):
    in_specs = (
        P(("batch", "seq"), "head"),
        P(("batch", "seq"), "head"),
        P(("batch", "seq"), None),
        P(("batch", "seq"), None),
        P("head", ("batch", "seq")),
        P("head", ("batch", "seq")),
        P("head"),
        P(),
        P("head", None),
    )
    out_specs = P(("batch", "seq", "head"), None)
    return jax.shard_map(body, mesh=mesh, in_specs=in_specs, out_specs=out_specs, check_vma=False)
```

time: 227 us -> 129 us (0.57)
  waiting for transfers between devices: 100 us -> 0 us
  Pallas kernels: 82.6 us -> 122 us
  between operations: 13.5 us -> 0.01 us
  blocking collectives: 10.1 us -> 0 us
  other arithmetic: 7.83 us -> 0 us
  starting transfers between devices: 4.1 us -> 0 us
    reduce_scatter x2 -> x0, waiting for transfers between devices: 83.8 us -> none  [body(): lax.psum_scatter(partial, 'head', scatter_dimension=0, tiled=True)]
    pallas_call x5 -> x1, Pallas kernels: 82.6 us -> 122 us  [body(): pl.pallas_call(functools.partial(mixer_kernel, (X, Y, S, groups, repeats)...]
    ppermute x3 -> x0, waiting for transfers between devices: 16.3 us -> none  [shifted(): lax.ppermute(value, axis, [(source, source + steps) for source in range(c...]
    unnamed x1 -> x0, blocking collectives: 10.1 us -> none
    convert_element_type x4 -> x0, other arithmetic: 7.14 us -> none  [the longest x1 3.69 us: body(): return (jnp.concatenate(parts, axis=0).astype(F32) * scale).astype(BF16)]
    ppermute x3 -> x0, starting transfers between devices: 3.88 us -> none  [shifted(): lax.ppermute(value, axis, [(source, source + steps) for source in range(c...]
    slice x3 -> x0, local copies, waits for them, and re-layouts: 2.35 us -> none  [the longest x2 1.55 us: body(): squares.append(square[0].reshape(shares, per_share // chunks))]
  transfers between devices with their start and end apart: 5 -> 0, of which waited for: 4 -> 0; matrix products, arithmetic and copies ran while one was open for 3% -> 0% of each run, Pallas kernels for 18% -> 0%
where the time goes in v1:
time: 129 us; the launch traced here: 128 us
  Pallas kernels  122 us (95%)
  local copies, waits for them, and re-layouts  6.17 us (5%)
    pallas_call x1, Pallas kernels, body(): pl.pallas_call(functools.partial(mixer_kernel, (X, Y, S, groups, repeats)...  122 us
    unnamed x1, local copies, waits for them, and re-layouts  3.4 us

profile of v1, /device:TPU:24, one launch (start us, length us, event | category | flops | bytes accessed | tf_op | source)
XLA Modules:
  0.0 128.3 jit_solution(7335396361911371323)
XLA Ops:
  0.0 0.8 dynamic_slice.3
  0.8 0.6 broadcast_in_dim.7.gain_ref
  1.4 0.7 broadcast_in_dim.6
  2.1 0.7 broadcast_in_dim_reshape.3.skip_ref
  2.8 122.1 %mixer.1 = bf16[512,2560]{1,0:T(8,128)(2,1)} custom-call(bf16[2048,1280]{1,0:T(8,128)(2,1)} %x_hbm.1, bf16[2048,1280]{1,0:T(8,128)(2,1)} %gate_hbm.1, bf16[2048,1024]{1,0:T(8,128)(2,1)} %b_hbm.1, bf16[2048,1024]{1,0:T(8,128)(2,1)} %c_hbm.1, f32[20,2048]{1,0:T(8,128)} %step_hbm.1, f32[20,2048]{1,0:T(8,128)} %log_hbm.1, ...), custom_call_target="tpu_custom_call" | custom-call | flops 18790481920 | bytes 20971520 | tf_op jit(solution)/shard_map/mixer/pallas_call | solution.py:468
  124.9 3.4 %copy.11 = bf16[512,2560]{1,0:T(8,128)(2,1)} copy(bf16[512,2560]{1,0:T(8,128)(2,1)} %mixer.1) | data formatting | bytes 5242880

commit v2 on v1

--- a/solution.py
+++ b/solution.py
@@ -67,7 +67,7 @@
 
 def mixer_kernel(
     plan, x_hbm, gate_hbm, b_hbm, c_hbm, step_hbm, log_hbm, skip_ref, gain_ref, w_hbm, out_hbm,
-    x, gate, b, c, step, log, w, stack, stack2, rows_ref, cols_ref, wcols_ref, prefix, base,
+    x, gate, b, c, step, log, w, stack, stack2, rows_ref, cols_ref, ends_ref, prefix, base,
     state_out, state_in, g_ref, part, squares, squares_in, first_a, first_b, second_a, second_b, stage,
     load_sem, out_sem, state_send, state_recv, square_send, square_recv,
     first_a_send, first_a_recv, first_b_send, first_b_recv,
@@ -87,6 +87,7 @@
     units = BLOCK // unit
     per_group = HEAD_COUNT // GROUPS
     every = pieces(channels, repeats)
+    first_gain = lax.axis_index("head") * len(every) if channels % LANES == 0 else 0
 
     me = lax.axis_index("head")
     z = lax.axis_index("seq")
@@ -134,7 +135,6 @@
     t_iota, s_iota = iotas(BLOCK, BLOCK)
     lower = jnp.where(s_iota <= t_iota, 1.0, 0.0)
     lower_b = lower.astype(BF16)
-    same_b = jnp.where(s_iota == t_iota, 1.0, 0.0).astype(BF16)
     stack[...] = jnp.zeros_like(stack)
     stack2[...] = jnp.ones_like(stack2)
     prefix[0] = jnp.zeros(prefix.shape[1:], F32)
@@ -157,12 +157,9 @@
     steps = stack2[...]
     rows_ref[...] = rows_all - jnp.log(steps)
     to_end = jnp.exp(rows_all[:, BLOCK - 1 : BLOCK] - rows_all) * steps
-    to_end_cols = 0.0
-    for part_of in split(to_end, 2):
-        to_end_cols = to_end_cols + dot(same_b, part_of, 1, 1)
+    ends_ref[...] = to_end
     for k in range(blocks):
         cols_ref[k] = cols_all[:, k * padded : (k + 1) * padded]
-        wcols_ref[k] = to_end_cols[:, k * padded : (k + 1) * padded]
 
     loads[2].wait()
     loads[3].wait()
@@ -176,12 +173,18 @@
             spot = pl.ds(pl.multiple_of(k * 8, 8), 8)
             following = pl.ds(pl.multiple_of(k * 8 + 8, 8), 8)
             end = cols_ref[k, BLOCK - 8 : BLOCK, :][7:8, :]
-            wide = wcols_ref[k]
+            ends = ends_ref[pl.ds(pl.multiple_of(k * padded, padded), padded), :]
+            turned = {}
             for p, start, width, of, group in some:
                 lanes = slice(start, start + width)
                 last = spread(end, of, width)
-                weighted = (x[row, lanes].astype(F32) * spread(wide, of, width)).astype(BF16)
-                new = dot(b[row, group * STATE : (group + 1) * STATE], weighted, 0, 0)
+                if group not in turned:
+                    turned[group] = b[row, group * STATE : (group + 1) * STATE].T.astype(F32)
+                scaled = [(turned[group] * ends[head : head + 1, :]).astype(BF16) for head in of]
+                both = dot(jnp.concatenate(scaled, axis=0), x[row, lanes], 1, 0)
+                new = both[:STATE]
+                if len(of) > 1:
+                    new = jnp.where(iotas(STATE, width)[1] < HEAD_DIM, new, both[STATE:])
                 prefix[k + 1, :, lanes] = jnp.exp(last) * prefix[k, :, lanes] + new
                 base[following, lanes] = base[spot, lanes] + last
             return carry
@@ -239,7 +242,10 @@
                 w_bottom = scores[group][mid:] * jnp.exp(jnp.minimum(column[mid:] - across, 0.0))
                 top = top + dot(w_top.astype(BF16), x_head[:mid], 1, 0)
                 bottom = bottom + dot(w_bottom.astype(BF16), x_head, 1, 0)
-            direct = skip_ref[:, lanes] * x_here.astype(F32)
+            gains = jnp.full((1, width), skip_ref[of[0]], F32)
+            if len(of) > 1:
+                gains = jnp.where(iotas(1, width)[1] < HEAD_DIM, gains, skip_ref[of[1]])
+            direct = gains * x_here.astype(F32)
             x[row, lanes] = jnp.concatenate([top + direct[:mid], bottom + direct[mid:]], axis=0).astype(BF16)
 
     def first_copy(buffer, send, recv, dx, dy, sub, row, columns, slot):
@@ -283,7 +289,7 @@
             v = gate[row, lanes].astype(F32)
             gated = (x[row, lanes].astype(F32) + across) * (v * (0.5 + 0.5 * jnp.tanh(0.5 * v)))
             total[width] = total.get(width, 0.0) + gated * gated
-            g_ref[:, lanes] = (gated * gain_ref[:, lanes]).astype(BF16)
+            g_ref[:, lanes] = (gated * gain_ref[pl.ds(first_gain + p, 1), :width]).astype(BF16)
         summed = jnp.zeros((8, BLOCK), F32)
         for width, value in total.items():
             for part_of in split(value, 2):
@@ -314,31 +320,25 @@
                 copy_squares(dx, dy, sub, index).start()
 
     loads[4].wait()
-    lag = max(1, (S - 1) * blocks // S) if S > 1 else 1
-    waits = jnp.where(z > 0, lax.max(z * blocks // S, 1) - 1, -1) if S > 1 else None
-
-    def main_step(i, carry):
-        @pl.when(i < blocks)
-        def _():
-            within(i)
-
+    waits = jnp.where(z > 0, lax.min(z * blocks // (S - 1), blocks - 1), -1) if S > 1 else None
+
+    def within_step(i, carry):
+        within(i)
         if S > 1:
             @pl.when(i == waits)
             def _():
                 pass_state()
 
-        @pl.when(i == lag)
-        def _():
-            loads[5].wait()
-            loads[6].wait()
-
-        @pl.when(i >= lag)
-        def _():
-            finish(i - lag)
-
         return carry
 
-    lax.fori_loop(0, blocks + lag, main_step, 0)
+    def finish_step(i, carry):
+        finish(i)
+        return carry
+
+    lax.fori_loop(0, blocks, within_step, 0)
+    loads[5].wait()
+    loads[6].wait()
+    lax.fori_loop(0, blocks, finish_step, 0)
 
     def second_copy(buffer, send, recv, dx, dy, slot, sub, row, columns):
         return pltpu.make_async_remote_copy(
@@ -459,15 +459,18 @@
     count = len(pieces(channels, repeats))
     padded = -(-heads // 8) * 8
     head_index = lax.axis_index("head")
-    skip = jnp.repeat(skip_gain, HEAD_DIM)[None, :]
-    gain = lax.dynamic_slice_in_dim(norm_gain, head_index * channels, channels)[None, :]
+    gain = norm_gain
+    if channels % LANES != 0:
+        gain = lax.dynamic_slice_in_dim(norm_gain, head_index * channels, channels)
+        gain = jnp.pad(gain, (0, count * LANES - channels))
+    gain = gain.reshape(-1, LANES)
     anywhere = pl.BlockSpec(memory_space=pl.ANY)
     vmem = pl.BlockSpec(memory_space=pltpu.VMEM)
     dma = pltpu.SemaphoreType.DMA
     x1, y1 = max(X - 1, 1), max(Y - 1, 1)
     return pl.pallas_call(
         functools.partial(mixer_kernel, (X, Y, S, groups, repeats)),
-        in_specs=[anywhere] * 6 + [vmem, vmem, anywhere],
+        in_specs=[anywhere] * 6 + [pl.BlockSpec(memory_space=pltpu.SMEM), vmem, anywhere],
         out_specs=anywhere,
         out_shape=jax.ShapeDtypeStruct((per_share, model), BF16),
         scratch_shapes=[
@@ -482,7 +485,7 @@
             pltpu.VMEM((blocks * padded, BLOCK), F32),
             pltpu.VMEM((blocks * padded, BLOCK), F32),
             pltpu.VMEM((blocks, BLOCK, padded), F32),
-            pltpu.VMEM((blocks, BLOCK, padded), F32),
+            pltpu.VMEM((blocks * padded, BLOCK), F32),
             pltpu.VMEM((blocks + 1, STATE, channels), F32),
             pltpu.VMEM(((blocks + 1) * 8, channels), F32),
             pltpu.VMEM((count, STATE, LANES), BF16),
@@ -518,7 +521,7 @@
         cost_estimate=pl.CostEstimate(
             flops=2 * tokens * channels * (model + 4 * BLOCK), bytes_accessed=tokens * channels * 8, transcendentals=0
         ),
-    )(ssm_input, gate_input, b_proj, c_proj, step_size, log_decay, skip, gain, out_weight)
+    )(ssm_input, gate_input, b_proj, c_proj, step_size, log_decay, skip_gain, gain, out_weight)
 
 
 def solution(mesh):

time: 129 us -> 122 us (0.946)
  Pallas kernels: 122 us -> 118 us
  local copies, waits for them, and re-layouts: 6.17 us -> 3.4 us
    pallas_call x1, Pallas kernels: 122 us -> 118 us  [body(): pl.pallas_call(functools.partial(mixer_kernel, (X, Y, S, groups, repeats)...]
    broadcast_in_dim x2 -> x0, local copies, waits for them, and re-layouts: 1.32 us -> none  [the longest x1 0.72 us: body(): skip = jnp.repeat(skip_gain, HEAD_DIM)[None, :]]
where the time goes in v2:
time: 122 us; the launch traced here: 121 us
  Pallas kernels  118 us (97%)
  local copies, waits for them, and re-layouts  3.4 us (3%)
    pallas_call x1, Pallas kernels, body(): pl.pallas_call(functools.partial(mixer_kernel, (X, Y, S, groups, repeats)...  118 us
    unnamed x1, local copies, waits for them, and re-layouts  3.4 us

profile of v2, /device:TPU:24, one launch (start us, length us, event | category | flops | bytes accessed | tf_op | source)
XLA Modules:
  0.0 121.4 jit_solution(13994031422236017918)
XLA Ops:
  0.0 118.0 %mixer.1 = bf16[512,2560]{1,0:T(8,128)(2,1)} custom-call(bf16[2048,1280]{1,0:T(8,128)(2,1)} %x_hbm.1, bf16[2048,1280]{1,0:T(8,128)(2,1)} %gate_hbm.1, bf16[2048,1024]{1,0:T(8,128)(2,1)} %b_hbm.1, bf16[2048,1024]{1,0:T(8,128)(2,1)} %c_hbm.1, f32[20,2048]{1,0:T(8,128)} %step_hbm.1, f32[20,2048]{1,0:T(8,128)} %log_hbm.1, f32[20]{0:T(128)} %skip_ref.1, ...), custom_call_target="tpu_custom_call" | custom-call | flops 18790481920 | bytes 20971520 | tf_op jit(solution)/shard_map/mixer/pallas_call | solution.py:471
  118.0 3.4 %copy.11 = bf16[512,2560]{1,0:T(8,128)(2,1)} copy(bf16[512,2560]{1,0:T(8,128)(2,1)} %mixer.1) | data formatting | bytes 5242880

commit v3 on v2

--- a/solution.py
+++ b/solution.py
@@ -438,6 +438,515 @@
                 state_copy(p).wait_send()
 
 
+def relay_plan(homes, S, blocks, passes):
+    count = len(homes)
+    span, hop = 7.5, 1.5
+    clock = [[0.0] * (2 * blocks + 5) for _ in range(S)]
+    for z in range(S):
+        now = 8.0
+        for at in range(blocks):
+            now = now + 1.4
+            if z > 0 and at == passes[z]:
+                now = max(now, 14.0 + 3.0 * z)
+            clock[z][at] = now
+        now = max(now, 14.0 + 3.0 * (S - 1))
+        for at in range(blocks, 2 * blocks):
+            now = now + 1.4
+            clock[z][at] = now
+        for at in range(2 * blocks, 2 * blocks + 5):
+            now = now + 6.0
+            clock[z][at] = now
+    arrival = [[None] * count for _ in range(S)]
+    taken = [{} for _ in range(S)]
+    plan = [{} for _ in range(S)]
+    order = [[] for _ in range(S)]
+    free = {}
+    for z in range(S):
+        for r, m in enumerate(m for m in range(count) if homes[m] == z):
+            arrival[z][m] = 2.5 + span * (r + 1)
+
+    def send(z, m, when, step):
+        begin = max(when, free.get((z, step), 0.0))
+        free[z, step] = begin + span
+        arrival[z + step][m] = begin + span + hop
+
+    late = [[] for _ in range(S)]
+    events = sorted((clock[z][at], z, at) for z in range(S) for at in range(2 * blocks + 5))
+    for when, z, at in events:
+        todo = plan[z].setdefault(at, [])
+        last = at == 2 * blocks + 4
+        if z == 0 or at > passes[z]:
+            for m in late[z]:
+                todo.append(("right", m))
+                send(z, m, when, 1)
+            late[z] = []
+        ready = [m for m in range(count) if m not in taken[z] and arrival[z][m] is not None]
+        ready = [m for m in ready if arrival[z][m] <= when + 0.2]
+        for m in sorted(ready, key=lambda m: arrival[z][m]):
+            taken[z][m] = at
+            order[z].append(m)
+            todo.append(("take", m))
+            todo.append(("side", m))
+            if z > 0 and homes[m] >= z:
+                todo.append(("left", m))
+                send(z, m, when, -1)
+            if z < S - 1 and homes[m] <= z:
+                if z == 0 or at > passes[z]:
+                    todo.append(("right", m))
+                    send(z, m, when, 1)
+                else:
+                    late[z].append(m)
+    for z in range(S):
+        rest = sorted(
+            (m for m in range(count) if m not in taken[z]), key=lambda m: (abs(homes[m] - z), m)
+        )
+        todo = plan[z].setdefault(2 * blocks + 4, [])
+        for m in rest:
+            order[z].append(m)
+            todo.append(("take", m))
+            todo.append(("side", m))
+            if z > 0 and homes[m] >= z:
+                todo.append(("left", m))
+            if z < S - 1 and homes[m] <= z:
+                todo.append(("right", m))
+    early = min(sum(1 for m in taken[z] if taken[z][m] < 2 * blocks) for z in range(S))
+    return plan, order, early
+
+
+def home_planes(count, S):
+    sizes = [count // S] * S
+    ends = [z for i in range(S) for z in ({i, S - 1 - i} if i < S - 1 - i else {i})][:S]
+    for i in range(count % S):
+        sizes[ends[i]] += 1
+    return [z for z in range(S) for _ in range(sizes[z])]
+
+
+def pair_kernel(
+    plan, x_hbm, gate_hbm, b_hbm, c_hbm, step_hbm, log_hbm, skip_ref, gain_ref, w_hbm, out_hbm,
+    x, gate, b, c, step, log, w, stack, stack2, rows_ref, cols_ref, ends_ref, prefix, base,
+    state_out, state_in, theirs, squares, squares_in, gated_in, sums_out, sums_in, stage, scale_ref,
+    load_sem, out_sem, state_send, state_recv, square_send, square_recv,
+    w_send, w_recv, gated_send, gated_recv, sums_send, sums_recv,
+):
+    X, Y, S, groups, repeats = plan
+    H = X * Y
+    tokens, channels = x.shape
+    model = w.shape[1]
+    heads = step.shape[0]
+    blocks = tokens // BLOCK
+    padded = stack.shape[0] // blocks
+    per_share = tokens // H
+    unit = UNIT
+    subs = per_share // unit
+    units = BLOCK // unit
+    share_blocks = per_share // BLOCK
+    per_group = HEAD_COUNT // GROUPS
+    every = pieces(channels, repeats)
+    first_gain = lax.axis_index("head") * len(every)
+    wide = 2 * LANES
+    count = model // wide
+    homes = home_planes(count, S)
+    passes = [min(zz * blocks // (S - 1), blocks - 1) for zz in range(S)]
+    tasks, order, early = relay_plan(homes, S, blocks, passes)
+
+    me = lax.axis_index("head")
+    z = lax.axis_index("seq")
+    core = lax.axis_index("batch")
+    gx = me % X
+    gy = me // X
+    to = lambda dx, dy: {"head": ((gy + dy) % Y) * X + (gx + dx) % X}
+    after = {"seq": lax.rem(z + 1, S)}
+    prior = {"seq": lax.max(z - 1, 0)}
+    sibling = {"batch": 1 - core}
+
+    offset = pl.multiple_of((me * heads // per_group) // groups * (groups * STATE), STATE)
+    loads = [
+        pltpu.make_async_copy(log_hbm, log, load_sem.at[0]),
+        pltpu.make_async_copy(step_hbm, step, load_sem.at[1]),
+        pltpu.make_async_copy(b_hbm.at[:, pl.ds(offset, groups * STATE)], b, load_sem.at[2]),
+        pltpu.make_async_copy(x_hbm, x, load_sem.at[3]),
+        pltpu.make_async_copy(c_hbm.at[:, pl.ds(offset, groups * STATE)], c, load_sem.at[4]),
+        pltpu.make_async_copy(gate_hbm, gate, load_sem.at[5]),
+        pltpu.make_async_copy(w_hbm, w, load_sem.at[6]),
+    ]
+    for load in loads:
+        load.start()
+
+    barrier = pltpu.get_barrier_semaphore()
+    for d in range(1, H):
+        pl.semaphore_signal(barrier, inc=1, device_id={"head": lax.rem(me + d, H)}, device_id_type=MESH)
+    pl.semaphore_signal(barrier, inc=1, device_id=sibling, device_id_type=MESH)
+
+    @pl.when(z > 0)
+    def _():
+        pl.semaphore_signal(barrier, inc=1, device_id=prior, device_id_type=MESH)
+
+    @pl.when(z < S - 1)
+    def _():
+        pl.semaphore_signal(barrier, inc=1, device_id=after, device_id_type=MESH)
+
+    pl.semaphore_wait(barrier, jnp.where(z > 0, 1, 0) + jnp.where(z < S - 1, 1, 0) + H)
+
+    def held(m, which):
+        return theirs.at[m, :, pl.ds(pl.multiple_of(which * LANES, LANES), LANES)]
+
+    def w_copy(m, kind):
+        source = held(m, core)
+        if kind == "first":
+            source = w_hbm.at[:, pl.ds(pl.multiple_of(m * wide + core * LANES, LANES), LANES)]
+        return pltpu.make_async_remote_copy(
+            src_ref=source, dst_ref=held(m, core),
+            send_sem=w_send.at[("first", "side", "left", "right").index(kind), m],
+            recv_sem=w_recv.at[m, core],
+            device_id={"first": to(1, 0), "side": sibling, "left": prior, "right": after}[kind],
+            device_id_type=MESH,
+        )
+
+    def w_arrival(m, which):
+        return pltpu.make_async_remote_copy(
+            src_ref=held(m, which), dst_ref=held(m, which), send_sem=w_send.at[0, m],
+            recv_sem=w_recv.at[m, which], device_id=sibling, device_id_type=MESH,
+        )
+
+    for zz in range(S):
+        @pl.when(z == zz)
+        def _(zz=zz):
+            for m in range(count):
+                if homes[m] == zz:
+                    w_copy(m, "first").start()
+
+    def relay(at):
+        for zz in range(S):
+            @pl.when(z == zz)
+            def _(zz=zz):
+                for slot, todo in tasks[zz].items():
+                    if not todo:
+                        continue
+
+                    @pl.when(at == slot)
+                    def _(todo=todo):
+                        for kind, m in todo:
+                            if kind == "take":
+                                w_arrival(m, core).wait_recv()
+                            else:
+                                w_copy(m, kind).start()
+
+    def chunk_at(position):
+        found = jnp.int32(0)
+        for zz in range(S):
+            for at in range(count):
+                found = jnp.where((z == zz) & (position == at), order[zz][at], found)
+        return found
+
+    def state_copy(p):
+        return pltpu.make_async_remote_copy(
+            src_ref=state_out.at[p], dst_ref=state_in.at[p], send_sem=state_send.at[p],
+            recv_sem=state_recv.at[p], device_id=after, device_id_type=MESH,
+        )
+
+    t_iota, s_iota = iotas(BLOCK, BLOCK)
+    lower = jnp.where(s_iota <= t_iota, 1.0, 0.0)
+    lower_b = lower.astype(BF16)
+    stack[...] = jnp.zeros_like(stack)
+    stack2[...] = jnp.ones_like(stack2)
+    prefix[0] = jnp.zeros(prefix.shape[1:], F32)
+    base[0:8] = jnp.zeros((8, channels), F32)
+    state_out[...] = jnp.zeros_like(state_out)
+
+    @pl.when(z == 0)
+    def _():
+        state_in[...] = jnp.zeros_like(state_in)
+
+    loads[0].wait()
+    loads[1].wait()
+    for k in range(blocks):
+        stack[k * padded : k * padded + heads, :] = log[:, k * BLOCK : (k + 1) * BLOCK]
+        stack2[k * padded : k * padded + heads, :] = step[:, k * BLOCK : (k + 1) * BLOCK]
+    rows_all, cols_all = 0.0, 0.0
+    for part_of in split(stack[...], 3):
+        rows_all = rows_all + dot(part_of, lower_b, 1, 1)
+        cols_all = cols_all + dot(lower_b, part_of, 1, 1)
+    steps = stack2[...]
+    rows_ref[...] = rows_all - jnp.log(steps)
+    to_end = jnp.exp(rows_all[:, BLOCK - 1 : BLOCK] - rows_all) * steps
+    ends_ref[...] = to_end
+    for k in range(blocks):
+        cols_ref[k] = cols_all[:, k * padded : (k + 1) * padded]
+
+    loads[2].wait()
+    loads[3].wait()
+    middle = (len(every) + 1) // 2
+    for some in (every[:middle], every[middle:]):
+        if not some:
+            continue
+
+        def state_step(k, carry, some=some):
+            row = pl.ds(pl.multiple_of(k * BLOCK, BLOCK), BLOCK)
+            spot = pl.ds(pl.multiple_of(k * 8, 8), 8)
+            following = pl.ds(pl.multiple_of(k * 8 + 8, 8), 8)
+            end = cols_ref[k, BLOCK - 8 : BLOCK, :][7:8, :]
+            ends = ends_ref[pl.ds(pl.multiple_of(k * padded, padded), padded), :]
+            turned = {}
+            for p, start, width, of, group in some:
+                lanes = slice(start, start + width)
+                last = spread(end, of, width)
+                if group not in turned:
+                    turned[group] = b[row, group * STATE : (group + 1) * STATE].T.astype(F32)
+                scaled = [(turned[group] * ends[head : head + 1, :]).astype(BF16) for head in of]
+                both = dot(jnp.concatenate(scaled, axis=0), x[row, lanes], 1, 0)
+                new = both[:STATE]
+                if len(of) > 1:
+                    new = jnp.where(iotas(STATE, width)[1] < HEAD_DIM, new, both[STATE:])
+                prefix[k + 1, :, lanes] = jnp.exp(last) * prefix[k, :, lanes] + new
+                base[following, lanes] = base[spot, lanes] + last
+            return carry
+
+        lax.fori_loop(0, blocks, state_step, 0)
+        if S > 1:
+            @pl.when(z == 0)
+            def _(some=some):
+                for p, start, width, of, group in some:
+                    state_out[p, :, :width] = prefix[blocks, :, start : start + width].astype(BF16)
+                    state_copy(p).start()
+
+    def pass_state():
+        for p, start, width, of, group in every:
+            lanes = slice(start, start + width)
+            state_copy(p).wait_recv()
+
+            @pl.when(z < S - 1)
+            def _():
+                grown = jnp.exp(base[blocks * 8 : blocks * 8 + 1, lanes]) * state_in[p, :, :width].astype(F32)
+                state_out[p, :, :width] = (grown + prefix[blocks, :, lanes]).astype(BF16)
+                state_copy(p).start()
+
+    def block_of(j):
+        mixed = j < 2 * share_blocks
+        rest = j - 2 * share_blocks
+        dx = jnp.where(mixed, 1 - j % 2, 1 - rest // share_blocks)
+        dy = jnp.where(mixed, 1, 0)
+        sub = jnp.where(mixed, j // 2, rest % share_blocks)
+        return dx, dy, sub
+
+    def within(k):
+        row = pl.ds(pl.multiple_of(k * BLOCK, BLOCK), BLOCK)
+        mid = BLOCK // 2
+        columns = cols_ref[k]
+        rows = rows_ref[pl.ds(pl.multiple_of(k * padded, padded), padded), :]
+        scores = {}
+        for p, start, width, of, group in every:
+            lanes = slice(start, start + width)
+            if group not in scores:
+                which = slice(group * STATE, (group + 1) * STATE)
+                scores[group] = dot(c[row, which], b[row, which], 1, 1) * lower
+            x_here = x[row, lanes]
+            lane = iotas(BLOCK, width)[1]
+            top, bottom = 0.0, 0.0
+            for i, head in enumerate(of):
+                kept = (lane >= i * HEAD_DIM) & (lane < (i + 1) * HEAD_DIM)
+                x_head = x_here if len(of) == 1 else jnp.where(kept, x_here, jnp.zeros_like(x_here))
+                column, across = columns[:, head : head + 1], rows[head : head + 1, :]
+                w_top = scores[group][:mid, :mid] * jnp.exp(
+                    jnp.minimum(column[:mid] - across[:, :mid], 0.0)
+                )
+                w_bottom = scores[group][mid:] * jnp.exp(jnp.minimum(column[mid:] - across, 0.0))
+                top = top + dot(w_top.astype(BF16), x_head[:mid], 1, 0)
+                bottom = bottom + dot(w_bottom.astype(BF16), x_head, 1, 0)
+            gains = jnp.full((1, width), skip_ref[of[0]], F32)
+            if len(of) > 1:
+                gains = jnp.where(iotas(1, width)[1] < HEAD_DIM, gains, skip_ref[of[1]])
+            direct = gains * x_here.astype(F32)
+            x[row, lanes] = jnp.concatenate([top + direct[:mid], bottom + direct[mid:]], axis=0).astype(BF16)
+
+    def row_of(dx, dy, sub):
+        owner = ((gy + dy) % Y) * X + (gx + dx) % X
+        return pl.multiple_of(owner * per_share + sub * unit, unit)
+
+    def copy_gated(dy, sub):
+        return pltpu.make_async_remote_copy(
+            src_ref=x.at[pl.ds(row_of(1, dy, sub), unit), :], dst_ref=gated_in.at[dy, sub],
+            send_sem=gated_send.at[dy, sub], recv_sem=gated_recv.at[dy, sub],
+            device_id=to(1, 0), device_id_type=MESH,
+        )
+
+    def copy_squares(dx, dy, sub, index):
+        slot = dx * Y + dy
+        return pltpu.make_async_remote_copy(
+            src_ref=squares.at[index], dst_ref=squares_in.at[slot, sub],
+            send_sem=square_send.at[slot, sub], recv_sem=square_recv.at[slot, sub],
+            device_id=to(dx, dy), device_id_type=MESH,
+        )
+
+    def copy_sums(sub, m):
+        return pltpu.make_async_remote_copy(
+            src_ref=sums_out.at[sub, m], dst_ref=sums_in.at[sub, m],
+            send_sem=sums_send.at[sub, m], recv_sem=sums_recv.at[sub, m],
+            device_id=to(0, 1), device_id_type=MESH,
+        )
+
+    def finish(j):
+        dx, dy, part_of_share = block_of(j)
+        k = row_of(dx, dy, part_of_share * units) // BLOCK
+        row = pl.ds(pl.multiple_of(k * BLOCK, BLOCK), BLOCK)
+        grow_all = jnp.exp(cols_ref[k])
+        before = jnp.exp(base[pl.ds(pl.multiple_of(k * 8, 8), 8), :])
+        total = {}
+        for p, start, width, of, group in every:
+            lanes = slice(start, start + width)
+            entering = prefix[k, :, lanes] + before[0:1, lanes] * state_in[p, :, :width].astype(F32)
+            moved = dot(c[row, group * STATE : (group + 1) * STATE], entering.astype(BF16), 1, 0)
+            across = spread(grow_all, of, width) * moved
+            v = gate[row, lanes].astype(F32)
+            gated = (x[row, lanes].astype(F32) + across) * (v * (0.5 + 0.5 * jnp.tanh(0.5 * v)))
+            total[width] = total.get(width, 0.0) + gated * gated
+            x[row, lanes] = (gated * gain_ref[pl.ds(first_gain + p, 1), :width]).astype(BF16)
+        summed = jnp.zeros((8, BLOCK), F32)
+        for width, value in total.items():
+            for part_of in split(value, 2):
+                summed = summed + dot(jnp.ones((8, width), BF16), part_of, 1, 1)
+        for u in range(units):
+            squares[k * units + u] = summed[:, u * unit : (u + 1) * unit]
+
+        @pl.when(dx > 0)
+        def _():
+            for u in range(units):
+                copy_gated(dy, part_of_share * units + u).start()
+
+        @pl.when(dx + dy > 0)
+        def _():
+            for u in range(units):
+                copy_squares(dx, dy, part_of_share * units + u, k * units + u).start()
+
+    def product(row, size, m, arrived):
+        columns = pl.ds(pl.multiple_of(m * wide, wide), wide)
+        return dot(x[pl.ds(row, size), :], w[:, columns], 1, 0) + dot(arrived, theirs[m], 1, 0)
+
+    loads[4].wait()
+    waits = jnp.where(z > 0, lax.min(z * blocks // (S - 1), blocks - 1), -1)
+
+    def within_step(i, carry):
+        within(i)
+
+        @pl.when(i == waits)
+        def _():
+            pass_state()
+
+        relay(i)
+        return carry
+
+    def finish_step(i, carry):
+        finish(i)
+        relay(i + blocks)
+        return carry
+
+    lax.fori_loop(0, blocks, within_step, 0)
+    loads[5].wait()
+    lax.fori_loop(0, blocks, finish_step, 0)
+    loads[6].wait()
+
+    def far_step(first, last, fresh, sub, carry):
+        if fresh:
+            copy_gated(1, sub).wait_recv()
+
+        def tile(position, carry):
+            m = chunk_at(position)
+
+            @pl.when(sub == 0)
+            def _():
+                w_arrival(m, 1 - core).wait_recv()
+
+            sums_out[sub, m] = product(row_of(0, 1, sub), unit, m, gated_in[1, sub]).astype(BF16)
+            copy_sums(sub, m).start()
+            return carry
+
+        lax.fori_loop(first, last, tile, 0)
+        if fresh:
+            relay(2 * blocks + sub)
+        return carry
+
+    lax.fori_loop(0, subs, functools.partial(far_step, 0, early, True), 0)
+    relay(2 * blocks + 4)
+    lax.fori_loop(0, subs, functools.partial(far_step, early, count, False), 0)
+
+    same_u = jnp.where(iotas(unit, unit)[0] == iotas(unit, unit)[1], 1.0, 0.0)
+
+    def scale_step(sub, carry):
+        summed = squares[me * subs + sub]
+        for dx in range(X):
+            for dy in range(Y):
+                if dx + dy > 0:
+                    copy_squares(dx, dy, sub, 0).wait_recv()
+                    summed = summed + squares_in[dx * Y + dy, sub]
+        column = dot(same_u, summed, 1, 1, HIGHEST)[:, 0:1]
+        there = pl.ds(pl.multiple_of(sub * unit, unit), unit)
+        scale_ref[there, :] = jnp.broadcast_to(lax.rsqrt(column / (HEAD_COUNT * HEAD_DIM) + epsilon), (unit, LANES))
+        return carry
+
+    lax.fori_loop(0, subs, scale_step, 0)
+
+    def out_copy(block, m):
+        there = pl.ds(pl.multiple_of(block * BLOCK, BLOCK), BLOCK)
+        columns = pl.ds(pl.multiple_of(m * wide, wide), wide)
+        return pltpu.make_async_copy(stage.at[there, columns], out_hbm.at[there, columns], out_sem.at[block, m])
+
+    def near_step(first, last, fresh, block, carry):
+        if fresh:
+            for u in range(units):
+                copy_gated(0, block * units + u).wait_recv()
+        there = pl.ds(pl.multiple_of(block * BLOCK, BLOCK), BLOCK)
+
+        def tile(position, carry):
+            m = chunk_at(position)
+            columns = pl.ds(pl.multiple_of(m * wide, wide), wide)
+            arrived = jnp.concatenate([gated_in[0, block * units + u] for u in range(units)], axis=0)
+            value = product(row_of(0, 0, block * units), BLOCK, m, arrived)
+            for u in range(units):
+                copy_sums(block * units + u, m).wait_recv()
+            value = value + jnp.concatenate([sums_in[block * units + u, m] for u in range(units)], axis=0).astype(F32)
+            scale = scale_ref[there, :]
+            stage[there, columns] = (value * jnp.concatenate([scale, scale], axis=1)).astype(BF16)
+            out_copy(block, m).start()
+            return carry
+
+        lax.fori_loop(first, last, tile, 0)
+        return carry
+
+    lax.fori_loop(0, share_blocks, functools.partial(near_step, 0, early, True), 0)
+    lax.fori_loop(0, share_blocks, functools.partial(near_step, early, count, False), 0)
+
+    def drain(m, carry):
+        for sub in range(subs):
+            copy_sums(sub, m).wait_send()
+        for block in range(share_blocks):
+            out_copy(block, m).wait()
+        w_copy(m, "side").wait_send()
+        return carry
+
+    lax.fori_loop(0, count, drain, 0)
+    for sub in range(subs):
+        for dy in range(Y):
+            copy_gated(dy, sub).wait_send()
+        for dx in range(X):
+            for dy in range(Y):
+                if dx + dy > 0:
+                    copy_squares(dx, dy, sub, 0).wait_send()
+    for zz in range(S):
+        @pl.when(z == zz)
+        def _(zz=zz):
+            for m in range(count):
+                if homes[m] == zz:
+                    w_copy(m, "first").wait_send()
+                if zz > 0 and homes[m] >= zz:
+                    w_copy(m, "left").wait_send()
+                if zz < S - 1 and homes[m] <= zz:
+                    w_copy(m, "right").wait_send()
+
+    @pl.when(z < S - 1)
+    def _():
+        for p, start, width, of, group in every:
+            state_copy(p).wait_send()
+
+
 def body(
     ssm_input, gate_input, b_proj, c_proj, step_size, log_decay, skip_gain, norm_gain, out_weight
 ):
@@ -468,28 +977,75 @@
     vmem = pl.BlockSpec(memory_space=pltpu.VMEM)
     dma = pltpu.SemaphoreType.DMA
     x1, y1 = max(X - 1, 1), max(Y - 1, 1)
+    side = [anywhere] * 6 + [pl.BlockSpec(memory_space=pltpu.SMEM), vmem, anywhere]
+    paired = (
+        X == 2 and Y == 2 and S > 1 and lax.axis_size("batch") == 2 and per_share % BLOCK == 0
+        and model % (2 * LANES) == 0 and channels % LANES == 0 and model // (2 * LANES) >= S
+        and per_share == 4 * UNIT
+    )
+    common = [
+        pltpu.VMEM((tokens, channels), BF16),
+        pltpu.VMEM((tokens, channels), BF16),
+        pltpu.VMEM((tokens, groups * STATE), BF16),
+        pltpu.VMEM((tokens, groups * STATE), BF16),
+        pltpu.VMEM((heads, tokens), F32),
+        pltpu.VMEM((heads, tokens), F32),
+        pltpu.VMEM((channels, model), BF16),
+        pltpu.VMEM((blocks * padded, BLOCK), F32),
+        pltpu.VMEM((blocks * padded, BLOCK), F32),
+        pltpu.VMEM((blocks * padded, BLOCK), F32),
+        pltpu.VMEM((blocks, BLOCK, padded), F32),
+        pltpu.VMEM((blocks * padded, BLOCK), F32),
+        pltpu.VMEM((blocks + 1, STATE, channels), F32),
+        pltpu.VMEM(((blocks + 1) * 8, channels), F32),
+        pltpu.VMEM((count, STATE, LANES), BF16),
+        pltpu.VMEM((count, STATE, LANES), BF16),
+    ]
+    cost = pl.CostEstimate(
+        flops=2 * tokens * channels * (model + 4 * BLOCK), bytes_accessed=tokens * channels * 8, transcendentals=0
+    )
+    params = pltpu.CompilerParams(
+        collective_id=0, has_side_effects=True, vmem_limit_bytes=62 * 1024 * 1024
+    )
+    if paired:
+        tiles = model // (2 * LANES)
+        return pl.pallas_call(
+            functools.partial(pair_kernel, (X, Y, S, groups, repeats)),
+            in_specs=side,
+            out_specs=anywhere,
+            out_shape=jax.ShapeDtypeStruct((per_share, model), BF16),
+            scratch_shapes=common + [
+                pltpu.VMEM((tiles, channels, 2 * LANES), BF16),
+                pltpu.VMEM((tokens // unit, 8, unit), F32),
+                pltpu.VMEM((H, subs, 8, unit), F32),
+                pltpu.VMEM((Y, subs, unit, channels), BF16),
+                pltpu.VMEM((subs, tiles, unit, 2 * LANES), BF16),
+                pltpu.VMEM((subs, tiles, unit, 2 * LANES), BF16),
+                pltpu.VMEM((per_share, model), BF16),
+                pltpu.VMEM((per_share, LANES), F32),
+                dma((7,)),
+                dma((per_share // BLOCK, tiles)),
+                dma((count,)),
+                dma((count,)),
+                dma((H, subs)),
+                dma((H, subs)),
+                dma((4, tiles)),
+                dma((tiles, 2)),
+                dma((Y, subs)),
+                dma((Y, subs)),
+                dma((subs, tiles)),
+                dma((subs, tiles)),
+            ],
+            compiler_params=params,
+            name="mixer_pair",
+            cost_estimate=cost,
+        )(ssm_input, gate_input, b_proj, c_proj, step_size, log_decay, skip_gain, gain, out_weight)
     return pl.pallas_call(
         functools.partial(mixer_kernel, (X, Y, S, groups, repeats)),
-        in_specs=[anywhere] * 6 + [pl.BlockSpec(memory_space=pltpu.SMEM), vmem, anywhere],
+        in_specs=side,
         out_specs=anywhere,
         out_shape=jax.ShapeDtypeStruct((per_share, model), BF16),
-        scratch_shapes=[
-            pltpu.VMEM((tokens, channels), BF16),
-            pltpu.VMEM((tokens, channels), BF16),
-            pltpu.VMEM((tokens, groups * STATE), BF16),
-            pltpu.VMEM((tokens, groups * STATE), BF16),
-            pltpu.VMEM((heads, tokens), F32),
-            pltpu.VMEM((heads, tokens), F32),
-            pltpu.VMEM((channels, model), BF16),
-            pltpu.VMEM((blocks * padded, BLOCK), F32),
-            pltpu.VMEM((blocks * padded, BLOCK), F32),
-            pltpu.VMEM((blocks * padded, BLOCK), F32),
-            pltpu.VMEM((blocks, BLOCK, padded), F32),
-            pltpu.VMEM((blocks * padded, BLOCK), F32),
-            pltpu.VMEM((blocks + 1, STATE, channels), F32),
-            pltpu.VMEM(((blocks + 1) * 8, channels), F32),
-            pltpu.VMEM((count, STATE, LANES), BF16),
-            pltpu.VMEM((count, STATE, LANES), BF16),
+        scratch_shapes=common + [
             pltpu.VMEM((BLOCK, channels), BF16),
             pltpu.VMEM((tokens, model), BF16),
             pltpu.VMEM((tokens // unit, 8, unit), F32),
@@ -514,13 +1070,9 @@
             dma((x1, subs)),
             dma((x1, subs)),
         ],
-        compiler_params=pltpu.CompilerParams(
-            collective_id=0, has_side_effects=True, vmem_limit_bytes=62 * 1024 * 1024
-        ),
+        compiler_params=params,
         name="mixer",
-        cost_estimate=pl.CostEstimate(
-            flops=2 * tokens * channels * (model + 4 * BLOCK), bytes_accessed=tokens * channels * 8, transcendentals=0
-        ),
+        cost_estimate=cost,
     )(ssm_input, gate_input, b_proj, c_proj, step_size, log_decay, skip_gain, gain, out_weight)
 
 

time: 122 us -> 118 us (0.967)
  Pallas kernels: 118 us -> 114 us
    pallas_call x1, Pallas kernels: 118 us -> 114 us  [body(): pl.pallas_call(functools.partial(pair_kernel, (X, Y, S, groups, repeats))...]
where the time goes in v3:
time: 118 us; the launch traced here: 117 us
  Pallas kernels  114 us (97%)
  local copies, waits for them, and re-layouts  3.4 us (3%)
    pallas_call x1, Pallas kernels, body(): pl.pallas_call(functools.partial(pair_kernel, (X, Y, S, groups, repeats))...  114 us
    unnamed x1, local copies, waits for them, and re-layouts  3.4 us

profile of v3, /device:TPU:24, one launch (start us, length us, event | category | flops | bytes accessed | tf_op | source)
XLA Modules:
  0.0 117.4 jit_solution(1938811276050939643)
XLA Ops:
  0.0 114.0 %mixer_pair.1 = bf16[512,2560]{1,0:T(8,128)(2,1)} custom-call(bf16[2048,1280]{1,0:T(8,128)(2,1)} %x_hbm.1, bf16[2048,1280]{1,0:T(8,128)(2,1)} %gate_hbm.1, bf16[2048,1024]{1,0:T(8,128)(2,1)} %b_hbm.1, bf16[2048,1024]{1,0:T(8,128)(2,1)} %c_hbm.1, f32[20,2048]{1,0:T(8,128)} %step_hbm.1, f32[20,2048]{1,0:T(8,128)} %log_hbm.1, f32[20]{0:T(128)} %skip_ref.1, ...), custom_call_target="tpu_custom_call" | custom-call | flops 18790481920 | bytes 20971520 | tf_op jit(solution)/shard_map/mixer_pair/pallas_call | solution.py:1012
  114.0 3.4 %copy.11 = bf16[512,2560]{1,0:T(8,128)(2,1)} copy(bf16[512,2560]{1,0:T(8,128)(2,1)} %mixer_pair.1) | data formatting | bytes 5242880

commit v4 on v3

--- a/solution.py
+++ b/solution.py
@@ -441,7 +441,7 @@
 def relay_plan(homes, S, blocks, passes):
     count = len(homes)
     span, hop = 7.5, 1.5
-    clock = [[0.0] * (2 * blocks + 5) for _ in range(S)]
+    clock = [[0.0] * (2 * blocks + 4) for _ in range(S)]
     for z in range(S):
         now = 8.0
         for at in range(blocks):
@@ -453,8 +453,8 @@
         for at in range(blocks, 2 * blocks):
             now = now + 1.4
             clock[z][at] = now
-        for at in range(2 * blocks, 2 * blocks + 5):
-            now = now + 6.0
+        for at in range(2 * blocks, 2 * blocks + 4):
+            now = now + 7.5
             clock[z][at] = now
     arrival = [[None] * count for _ in range(S)]
     taken = [{} for _ in range(S)]
@@ -471,10 +471,9 @@
         arrival[z + step][m] = begin + span + hop
 
     late = [[] for _ in range(S)]
-    events = sorted((clock[z][at], z, at) for z in range(S) for at in range(2 * blocks + 5))
+    events = sorted((clock[z][at], z, at) for z in range(S) for at in range(2 * blocks + 4))
     for when, z, at in events:
         todo = plan[z].setdefault(at, [])
-        last = at == 2 * blocks + 4
         if z == 0 or at > passes[z]:
             for m in late[z]:
                 todo.append(("right", m))
@@ -496,21 +495,21 @@
                     send(z, m, when, 1)
                 else:
                     late[z].append(m)
+    final = [{} for _ in range(S)]
     for z in range(S):
-        rest = sorted(
-            (m for m in range(count) if m not in taken[z]), key=lambda m: (abs(homes[m] - z), m)
-        )
-        todo = plan[z].setdefault(2 * blocks + 4, [])
-        for m in rest:
+        rest = [m for m in range(count) if m not in taken[z]]
+        for m in sorted(rest, key=lambda m: (abs(homes[m] - z), m)):
+            todo = final[z].setdefault(len(order[z]), [("take", m), ("side", m)])
             order[z].append(m)
-            todo.append(("take", m))
-            todo.append(("side", m))
             if z > 0 and homes[m] >= z:
                 todo.append(("left", m))
             if z < S - 1 and homes[m] <= z:
                 todo.append(("right", m))
-    early = min(sum(1 for m in taken[z] if taken[z][m] < 2 * blocks) for z in range(S))
-    return plan, order, early
+    ready = [
+        min(sum(1 for m in taken[z] if taken[z][m] < at) for z in range(S))
+        for at in range(2 * blocks, 2 * blocks + 5)
+    ]
+    return plan, final, order, ready
 
 
 def home_planes(count, S):
@@ -547,7 +546,7 @@
     count = model // wide
     homes = home_planes(count, S)
     passes = [min(zz * blocks // (S - 1), blocks - 1) for zz in range(S)]
-    tasks, order, early = relay_plan(homes, S, blocks, passes)
+    tasks, final, order, ready = relay_plan(homes, S, blocks, passes)
 
     me = lax.axis_index("head")
     z = lax.axis_index("seq")
@@ -615,7 +614,7 @@
                 if homes[m] == zz:
                     w_copy(m, "first").start()
 
-    def relay(at):
+    def relay(at, tasks=tasks):
         for zz in range(S):
             @pl.when(z == zz)
             def _(zz=zz):
@@ -844,10 +843,7 @@
     lax.fori_loop(0, blocks, finish_step, 0)
     loads[6].wait()
 
-    def far_step(first, last, fresh, sub, carry):
-        if fresh:
-            copy_gated(1, sub).wait_recv()
-
+    def far_tiles(sub, first, last):
         def tile(position, carry):
             m = chunk_at(position)
 
@@ -860,13 +856,40 @@
             return carry
 
         lax.fori_loop(first, last, tile, 0)
-        if fresh:
-            relay(2 * blocks + sub)
-        return carry
-
-    lax.fori_loop(0, subs, functools.partial(far_step, 0, early, True), 0)
-    relay(2 * blocks + 4)
-    lax.fori_loop(0, subs, functools.partial(far_step, early, count, False), 0)
+
+    def of_step(at):
+        found = jnp.int32(ready[0])
+        for i in range(1, subs + 1):
+            found = jnp.where(at >= i, jnp.int32(ready[i]), found)
+        return found
+
+    def far_step(sub, carry):
+        copy_gated(1, sub).wait_recv()
+        known = of_step(sub)
+        far_tiles(sub, 0, known)
+        relay(2 * blocks + sub)
+        fresh = of_step(sub + 1)
+
+        def older(other, carry):
+            far_tiles(other, known, fresh)
+            return carry
+
+        lax.fori_loop(0, sub + 1, older, 0)
+        return carry
+
+    lax.fori_loop(0, subs, far_step, 0)
+
+    def late_step(position, carry):
+        relay(position, final)
+
+        def older(other, carry):
+            far_tiles(other, position, position + 1)
+            return carry
+
+        lax.fori_loop(0, subs, older, 0)
+        return carry
+
+    lax.fori_loop(ready[subs], count, late_step, 0)
 
     same_u = jnp.where(iotas(unit, unit)[0] == iotas(unit, unit)[1], 1.0, 0.0)
 
@@ -889,30 +912,36 @@
         columns = pl.ds(pl.multiple_of(m * wide, wide), wide)
         return pltpu.make_async_copy(stage.at[there, columns], out_hbm.at[there, columns], out_sem.at[block, m])
 
-    def near_step(first, last, fresh, block, carry):
-        if fresh:
-            for u in range(units):
-                copy_gated(0, block * units + u).wait_recv()
+    def near_tile(block, position):
         there = pl.ds(pl.multiple_of(block * BLOCK, BLOCK), BLOCK)
+        m = chunk_at(position)
+        columns = pl.ds(pl.multiple_of(m * wide, wide), wide)
+        arrived = jnp.concatenate([gated_in[0, block * units + u] for u in range(units)], axis=0)
+        value = product(row_of(0, 0, block * units), BLOCK, m, arrived)
+        for u in range(units):
+            copy_sums(block * units + u, m).wait_recv()
+        value = value + jnp.concatenate([sums_in[block * units + u, m] for u in range(units)], axis=0).astype(F32)
+        scale = scale_ref[there, :]
+        stage[there, columns] = (value * jnp.concatenate([scale, scale], axis=1)).astype(BF16)
+        out_copy(block, m).start()
+
+    def near_step(block, carry):
+        for u in range(units):
+            copy_gated(0, block * units + u).wait_recv()
 
         def tile(position, carry):
-            m = chunk_at(position)
-            columns = pl.ds(pl.multiple_of(m * wide, wide), wide)
-            arrived = jnp.concatenate([gated_in[0, block * units + u] for u in range(units)], axis=0)
-            value = product(row_of(0, 0, block * units), BLOCK, m, arrived)
-            for u in range(units):
-                copy_sums(block * units + u, m).wait_recv()
-            value = value + jnp.concatenate([sums_in[block * units + u, m] for u in range(units)], axis=0).astype(F32)
-            scale = scale_ref[there, :]
-            stage[there, columns] = (value * jnp.concatenate([scale, scale], axis=1)).astype(BF16)
-            out_copy(block, m).start()
+            near_tile(block, position)
             return carry
 
-        lax.fori_loop(first, last, tile, 0)
-        return carry
-
-    lax.fori_loop(0, share_blocks, functools.partial(near_step, 0, early, True), 0)
-    lax.fori_loop(0, share_blocks, functools.partial(near_step, early, count, False), 0)
+        lax.fori_loop(0, ready[subs], tile, 0)
+        return carry
+
+    def last_step(i, carry):
+        near_tile(i % share_blocks, ready[subs] + i // share_blocks)
+        return carry
+
+    lax.fori_loop(0, share_blocks, near_step, 0)
+    lax.fori_loop(0, share_blocks * (count - ready[subs]), last_step, 0)
 
     def drain(m, carry):
         for sub in range(subs):

time: 118 us -> 105 us (0.89)
  Pallas kernels: 114 us -> 101 us
    pallas_call x1, Pallas kernels: 114 us -> 101 us  [body(): pl.pallas_call(functools.partial(pair_kernel, (X, Y, S, groups, repeats))...]
where the time goes in v4:
time: 105 us
  Pallas kernels  101 us (96%)
  local copies, waits for them, and re-layouts  3.4 us (3%)
    pallas_call x1, Pallas kernels, body(): pl.pallas_call(functools.partial(pair_kernel, (X, Y, S, groups, repeats))...  101 us
    unnamed x1, local copies, waits for them, and re-layouts  3.4 us

profile of v4, /device:TPU:24, one launch (start us, length us, event | category | flops | bytes accessed | tf_op | source)
XLA Modules:
  0.0 104.6 jit_solution(5039754287816578998)
XLA Ops:
  0.0 101.2 %mixer_pair.1 = bf16[512,2560]{1,0:T(8,128)(2,1)} custom-call(bf16[2048,1280]{1,0:T(8,128)(2,1)} %x_hbm.1, bf16[2048,1280]{1,0:T(8,128)(2,1)} %gate_hbm.1, bf16[2048,1024]{1,0:T(8,128)(2,1)} %b_hbm.1, bf16[2048,1024]{1,0:T(8,128)(2,1)} %c_hbm.1, f32[20,2048]{1,0:T(8,128)} %step_hbm.1, f32[20,2048]{1,0:T(8,128)} %log_hbm.1, f32[20]{0:T(128)} %skip_ref.1, ...), custom_call_target="tpu_custom_call" | custom-call | flops 18790481920 | bytes 20971520 | tf_op jit(solution)/shard_map/mixer_pair/pallas_call | solution.py:1041
  101.2 3.4 %copy.11 = bf16[512,2560]{1,0:T(8,128)(2,1)} copy(bf16[512,2560]{1,0:T(8,128)(2,1)} %mixer_pair.1) | data formatting | bytes 5242880

commit v5 on v4

--- a/solution.py
+++ b/solution.py
@@ -438,23 +438,22 @@
                 state_copy(p).wait_send()
 
 
-def relay_plan(homes, S, blocks, passes):
+def relay_plan(homes, S, blocks, lag, passes):
     count = len(homes)
     span, hop = 7.5, 1.5
-    clock = [[0.0] * (2 * blocks + 4) for _ in range(S)]
+    steps = blocks + lag
+    clock = [[0.0] * (steps + 4) for _ in range(S)]
     for z in range(S):
-        now = 8.0
-        for at in range(blocks):
-            now = now + 1.4
+        now = 8.5
+        for at in range(steps):
+            now = now + (1.4 if at < blocks else 0.0) + (1.1 if at >= lag else 0.0)
             if z > 0 and at == passes[z]:
-                now = max(now, 14.0 + 3.0 * z)
+                now = max(now, 9.0 + 3.2 * z)
+            if at == lag - 1:
+                now = max(now, 9.0 + 3.2 * (S - 1))
             clock[z][at] = now
-        now = max(now, 14.0 + 3.0 * (S - 1))
-        for at in range(blocks, 2 * blocks):
-            now = now + 1.4
-            clock[z][at] = now
-        for at in range(2 * blocks, 2 * blocks + 4):
-            now = now + 7.5
+        for at in range(steps, steps + 4):
+            now = now + (3.0 if at == steps else 7.5)
             clock[z][at] = now
     arrival = [[None] * count for _ in range(S)]
     taken = [{} for _ in range(S)]
@@ -471,7 +470,7 @@
         arrival[z + step][m] = begin + span + hop
 
     late = [[] for _ in range(S)]
-    events = sorted((clock[z][at], z, at) for z in range(S) for at in range(2 * blocks + 4))
+    events = sorted((clock[z][at], z, at) for z in range(S) for at in range(steps + 4))
     for when, z, at in events:
         todo = plan[z].setdefault(at, [])
         if z == 0 or at > passes[z]:
@@ -507,7 +506,7 @@
                 todo.append(("right", m))
     ready = [
         min(sum(1 for m in taken[z] if taken[z][m] < at) for z in range(S))
-        for at in range(2 * blocks, 2 * blocks + 5)
+        for at in range(steps, steps + 5)
     ]
     return plan, final, order, ready
 
@@ -523,7 +522,7 @@
 def pair_kernel(
     plan, x_hbm, gate_hbm, b_hbm, c_hbm, step_hbm, log_hbm, skip_ref, gain_ref, w_hbm, out_hbm,
     x, gate, b, c, step, log, w, stack, stack2, rows_ref, cols_ref, ends_ref, prefix, base,
-    state_out, state_in, theirs, squares, squares_in, gated_in, sums_out, sums_in, stage, scale_ref,
+    state_out, state_in, theirs, squares, squares_in, gated_in, sums_out, sums_in, stage, scale_ref, own_ref,
     load_sem, out_sem, state_send, state_recv, square_send, square_recv,
     w_send, w_recv, gated_send, gated_recv, sums_send, sums_recv,
 ):
@@ -545,8 +544,9 @@
     wide = 2 * LANES
     count = model // wide
     homes = home_planes(count, S)
-    passes = [min(zz * blocks // (S - 1), blocks - 1) for zz in range(S)]
-    tasks, final, order, ready = relay_plan(homes, S, blocks, passes)
+    passes = [max(zz * blocks // S - 1, 0) for zz in range(S)]
+    lag = passes[-1] + 1
+    tasks, final, order, ready = relay_plan(homes, S, blocks, lag, passes)
 
     me = lax.axis_index("head")
     z = lax.axis_index("seq")
@@ -568,7 +568,7 @@
         pltpu.make_async_copy(gate_hbm, gate, load_sem.at[5]),
         pltpu.make_async_copy(w_hbm, w, load_sem.at[6]),
     ]
-    for load in loads:
+    for load in loads[:4]:
         load.start()
 
     barrier = pltpu.get_barrier_semaphore()
@@ -674,39 +674,38 @@
 
     loads[2].wait()
     loads[3].wait()
-    middle = (len(every) + 1) // 2
-    for some in (every[:middle], every[middle:]):
-        if not some:
-            continue
-
-        def state_step(k, carry, some=some):
-            row = pl.ds(pl.multiple_of(k * BLOCK, BLOCK), BLOCK)
-            spot = pl.ds(pl.multiple_of(k * 8, 8), 8)
-            following = pl.ds(pl.multiple_of(k * 8 + 8, 8), 8)
-            end = cols_ref[k, BLOCK - 8 : BLOCK, :][7:8, :]
-            ends = ends_ref[pl.ds(pl.multiple_of(k * padded, padded), padded), :]
-            turned = {}
+    for load in loads[4:]:
+        load.start()
+    for first in range(0, len(every), 2):
+        some = every[first : first + 2]
+
+        def state_step(pair, carry, some=some):
+            for k in (2 * pair, 2 * pair + 1):
+                row = pl.ds(pl.multiple_of(k * BLOCK, BLOCK), BLOCK)
+                spot = pl.ds(pl.multiple_of(k * 8, 8), 8)
+                following = pl.ds(pl.multiple_of(k * 8 + 8, 8), 8)
+                end = cols_ref[k, BLOCK - 8 : BLOCK, :][7:8, :]
+                ends = ends_ref[pl.ds(pl.multiple_of(k * padded, padded), padded), :]
+                turned = {}
+                for p, start, width, of, group in some:
+                    lanes = slice(start, start + width)
+                    last = spread(end, of, width)
+                    if group not in turned:
+                        turned[group] = b[row, group * STATE : (group + 1) * STATE].T.astype(F32)
+                    scaled = [(turned[group] * ends[head : head + 1, :]).astype(BF16) for head in of]
+                    both = dot(jnp.concatenate(scaled, axis=0), x[row, lanes], 1, 0)
+                    new = jnp.where(iotas(STATE, width)[1] < HEAD_DIM, both[:STATE], both[STATE:])
+                    prefix[k + 1, :, lanes] = jnp.exp(last) * prefix[k, :, lanes] + new
+                    base[following, lanes] = base[spot, lanes] + last
+            return carry
+
+        lax.fori_loop(0, blocks // 2, state_step, 0)
+
+        @pl.when(z == 0)
+        def _(some=some):
             for p, start, width, of, group in some:
-                lanes = slice(start, start + width)
-                last = spread(end, of, width)
-                if group not in turned:
-                    turned[group] = b[row, group * STATE : (group + 1) * STATE].T.astype(F32)
-                scaled = [(turned[group] * ends[head : head + 1, :]).astype(BF16) for head in of]
-                both = dot(jnp.concatenate(scaled, axis=0), x[row, lanes], 1, 0)
-                new = both[:STATE]
-                if len(of) > 1:
-                    new = jnp.where(iotas(STATE, width)[1] < HEAD_DIM, new, both[STATE:])
-                prefix[k + 1, :, lanes] = jnp.exp(last) * prefix[k, :, lanes] + new
-                base[following, lanes] = base[spot, lanes] + last
-            return carry
-
-        lax.fori_loop(0, blocks, state_step, 0)
-        if S > 1:
-            @pl.when(z == 0)
-            def _(some=some):
-                for p, start, width, of, group in some:
-                    state_out[p, :, :width] = prefix[blocks, :, start : start + width].astype(BF16)
-                    state_copy(p).start()
+                state_out[p, :, :width] = prefix[blocks, :, start : start + width].astype(BF16)
+                state_copy(p).start()
 
     def pass_state():
         for p, start, width, of, group in every:
@@ -783,9 +782,13 @@
             device_id=to(0, 1), device_id_type=MESH,
         )
 
+    def first_row(j):
+        dx, dy, part_of_share = block_of(j)
+        return row_of(dx, dy, part_of_share * units)
+
     def finish(j):
         dx, dy, part_of_share = block_of(j)
-        k = row_of(dx, dy, part_of_share * units) // BLOCK
+        k = first_row(j) // BLOCK
         row = pl.ds(pl.multiple_of(k * BLOCK, BLOCK), BLOCK)
         grow_all = jnp.exp(cols_ref[k])
         before = jnp.exp(base[pl.ds(pl.multiple_of(k * 8, 8), 8), :])
@@ -821,26 +824,27 @@
         return dot(x[pl.ds(row, size), :], w[:, columns], 1, 0) + dot(arrived, theirs[m], 1, 0)
 
     loads[4].wait()
-    waits = jnp.where(z > 0, lax.min(z * blocks // (S - 1), blocks - 1), -1)
-
-    def within_step(i, carry):
-        within(i)
-
-        @pl.when(i == waits)
+    def main_step(i, carry):
+        @pl.when(i == lag)
+        def _():
+            loads[5].wait()
+
+        @pl.when(i >= lag)
+        def _():
+            finish(i - lag)
+
+        @pl.when(i < blocks)
+        def _():
+            within(first_row(i) // BLOCK)
+
+        @pl.when((z > 0) & (i == lax.max(z * blocks // S - 1, 0)))
         def _():
             pass_state()
 
         relay(i)
         return carry
 
-    def finish_step(i, carry):
-        finish(i)
-        relay(i + blocks)
-        return carry
-
-    lax.fori_loop(0, blocks, within_step, 0)
-    loads[5].wait()
-    lax.fori_loop(0, blocks, finish_step, 0)
+    lax.fori_loop(0, blocks + lag, main_step, 0)
     loads[6].wait()
 
     def far_tiles(sub, first, last):
@@ -867,7 +871,7 @@
         copy_gated(1, sub).wait_recv()
         known = of_step(sub)
         far_tiles(sub, 0, known)
-        relay(2 * blocks + sub)
+        relay(blocks + lag + sub)
         fresh = of_step(sub + 1)
 
         def older(other, carry):
@@ -875,6 +879,15 @@
             return carry
 
         lax.fori_loop(0, sub + 1, older, 0)
+
+        def ahead(i, carry):
+            block, m = i // count, i % count
+            columns = pl.ds(pl.multiple_of(m * wide, wide), wide)
+            own_ref[block, m] = dot(x[pl.ds(row_of(0, 0, block * units), BLOCK), :], w[:, columns], 1, 0)
+            return carry
+
+        share = -(-share_blocks * count // subs)
+        lax.fori_loop(sub * share, lax.min((sub + 1) * share, share_blocks * count), ahead, 0)
         return carry
 
     lax.fori_loop(0, subs, far_step, 0)
@@ -917,7 +930,7 @@
         m = chunk_at(position)
         columns = pl.ds(pl.multiple_of(m * wide, wide), wide)
         arrived = jnp.concatenate([gated_in[0, block * units + u] for u in range(units)], axis=0)
-        value = product(row_of(0, 0, block * units), BLOCK, m, arrived)
+        value = own_ref[block, m] + dot(arrived, theirs[m], 1, 0)
         for u in range(units):
             copy_sums(block * units + u, m).wait_recv()
         value = value + jnp.concatenate([sums_in[block * units + u, m] for u in range(units)], axis=0).astype(F32)
@@ -1010,7 +1023,7 @@
     paired = (
         X == 2 and Y == 2 and S > 1 and lax.axis_size("batch") == 2 and per_share % BLOCK == 0
         and model % (2 * LANES) == 0 and channels % LANES == 0 and model // (2 * LANES) >= S
-        and per_share == 4 * UNIT
+        and per_share == 4 * UNIT and blocks % 2 == 0
     )
     common = [
         pltpu.VMEM((tokens, channels), BF16),
@@ -1052,6 +1065,7 @@
                 pltpu.VMEM((subs, tiles, unit, 2 * LANES), BF16),
                 pltpu.VMEM((per_share, model), BF16),
                 pltpu.VMEM((per_share, LANES), F32),
+                pltpu.VMEM((per_share // BLOCK, tiles, BLOCK, 2 * LANES), F32),
                 dma((7,)),
                 dma((per_share // BLOCK, tiles)),
                 dma((count,)),

time: 105 us -> 103 us (0.981)
  Pallas kernels: 101 us -> 99.5 us
    pallas_call x1, Pallas kernels: 101 us -> 99.5 us  [body(): pl.pallas_call(functools.partial(pair_kernel, (X, Y, S, groups, repeats))...]
where the time goes in v5:
time: 103 us
  Pallas kernels  99.5 us (97%)
  local copies, waits for them, and re-layouts  3.4 us (3%)
    pallas_call x1, Pallas kernels, body(): pl.pallas_call(functools.partial(pair_kernel, (X, Y, S, groups, repeats))...  99.5 us
    unnamed x1, local copies, waits for them, and re-layouts  3.4 us

profile of v5, /device:TPU:24, one launch (start us, length us, event | category | flops | bytes accessed | tf_op | source)
XLA Modules:
  0.0 102.9 jit_solution(14542143387563635)
XLA Ops:
  0.0 99.5 %mixer_pair.1 = bf16[512,2560]{1,0:T(8,128)(2,1)} custom-call(bf16[2048,1280]{1,0:T(8,128)(2,1)} %x_hbm.1, bf16[2048,1280]{1,0:T(8,128)(2,1)} %gate_hbm.1, bf16[2048,1024]{1,0:T(8,128)(2,1)} %b_hbm.1, bf16[2048,1024]{1,0:T(8,128)(2,1)} %c_hbm.1, f32[20,2048]{1,0:T(8,128)} %step_hbm.1, f32[20,2048]{1,0:T(8,128)} %log_hbm.1, f32[20]{0:T(128)} %skip_ref.1, ...), custom_call_target="tpu_custom_call" | custom-call | flops 18790481920 | bytes 20971520 | tf_op jit(solution)/shard_map/mixer_pair/pallas_call | solution.py:1054
  99.5 3.4 %copy.11 = bf16[512,2560]{1,0:T(8,128)(2,1)} copy(bf16[512,2560]{1,0:T(8,128)(2,1)} %mixer_pair.1) | data formatting | bytes 5242880
